TPU v7x, 32 devices: a whole 2x2x4 slice. The times are simulated.
32 devices in a mesh: gx: 4 (over y, x), gy: 8 (over z, core).
Axes of the slice: x: 2, y: 2, z: 4, core: 2. Of those that a mesh axis runs over, the one named last changes fastest.
Arguments:
- density: float32 [128, 256, 256], P('gx', 'gy'), may hold values from -6 to 6
- flux_east: float32 [128, 256, 256], P('gx', 'gy'), may hold values from -6 to 6
- flux_north: float32 [128, 256, 256], P('gx', 'gy'), may hold values from -6 to 6
- flux_up: float32 [128, 256, 256], P('gx', 'gy'), may hold values from -6 to 6
- theta_pert: float32 [128, 256, 256], P('gx', 'gy'), may hold values from -2 to 4
- sound_coef: bfloat16 [128, 256, 256], P('gx', 'gy'), may hold values from 0.5 to 2
- vert_inverse: float32 [512, 512], replicated, may hold values from -1 to 1
Outputs:
- density_new: float32 [128, 256, 256], P('gx', 'gy')
- east_new: float32 [128, 256, 256], P('gx', 'gy')
- north_new: float32 [128, 256, 256], P('gx', 'gy')
- upward_new: float32 [128, 256, 256], P('gx', 'gy')
- theta_new: float32 [128, 256, 256], P('gx', 'gy')
All inputs are finite; a program needn't handle non-finite values.
Results may differ from a plain program's by a relative error of at most 0.0003.
Values sent between devices are 32-bit elements; how exact they have to be, the bound alone decides.
No kernel may reach another device: no remote copies, remote signals or barrier semaphores. Data moves between devices by JAX's collectives and lax.ppermute only.
A program may use at most 64 MiB of HBM per device.

v0:
```python
import jax
import jax.numpy as jnp
from jax import lax
from jax.experimental import pallas as pl
from jax.experimental.pallas import tpu as pltpu
from jax.sharding import PartitionSpec as P

SUBSTEPS = 6

courant = 0.45
damping = 0.1

MIB = 1024 * 1024
ROWS = 8
TILE = 8

ROUTES = (("gy", 1), ("gx", 1), ("gx", 0), ("gy", 0))


def paired(block, axis, odd):
    count = lax.axis_size(axis)
    route = []
    for low in range(odd, count + odd, 2):
        a, b = low % count, (low + 1) % count
        route += [(a, b), (b, a)]
    return lax.ppermute(block, axis, route)


def is_even(axis):
    return lax.axis_index(axis) % 2 == 0


def put_edges(first_x, last_x, first_y, last_y, outs):
    even_x, even_y = is_even("gx"), is_even("gy")
    outs[0][...] = jnp.where(even_y, first_y, last_y)
    outs[1][...] = jnp.where(even_x, first_x, last_x)
    outs[2][...] = jnp.where(even_x, last_x, first_x)
    outs[3][...] = jnp.where(even_y, last_y, first_y)


EVERY = slice(None)


def west_of(halo, rows=EVERY):
    return jnp.where(is_even("gx"), halo[1][rows, :], halo[2][rows, :])


def east_of(halo, rows=EVERY):
    return jnp.where(is_even("gx"), halo[2][rows, :], halo[1][rows, :])


def south_of(halo, rows=EVERY):
    return jnp.where(is_even("gy"), halo[0][rows, :], halo[3][rows, :])


def north_of(halo, rows=EVERY):
    return jnp.where(is_even("gy"), halo[3][rows, :], halo[0][rows, :])


def split(value):
    high = value.astype(jnp.bfloat16)
    low = (value - high.astype(jnp.float32)).astype(jnp.bfloat16)
    return high, low


def product(value, mat_ref):
    high, low = split(value)
    terms = jnp.concatenate([high, low, high], axis=1)
    return jnp.dot(terms, mat_ref[...], preferred_element_type=jnp.float32)


def before(rows, first):
    return jnp.concatenate([first, rows[:-1]], axis=0)


def after(rows, last):
    return jnp.concatenate([rows[1:], last], axis=0)


def level_difference(upward):
    lane = lax.broadcasted_iota(jnp.int32, upward.shape, 1)
    below = jnp.where(lane == 0, 0.0, pltpu.roll(upward, 1, 1))
    return upward - below


def first_edges_kernel(nx, ny, th_hbm, coef_hbm, u_hbm, v_hbm, *refs):
    outs, coef_out = refs[:4], refs[4]
    th_x, th_y, coef_x, coef_y, u_x, v_y, sems = refs[5:]
    copies = []

    def fetch(src, dst):
        copies.append(pltpu.make_async_copy(src, dst, sems.at[len(copies)]))
        copies[-1].start()

    for side, i in enumerate((0, nx - 1)):
        fetch(th_hbm.at[i], th_x.at[side])
        fetch(coef_hbm.at[i], coef_x.at[side])
    fetch(u_hbm.at[0], u_x)
    for side, j in enumerate((0, ny - TILE)):
        fetch(th_hbm.at[:, pl.ds(j, TILE), :], th_y.at[side])
        fetch(coef_hbm.at[:, pl.ds(j, TILE), :], coef_y.at[side])
    fetch(v_hbm.at[:, pl.ds(0, TILE), :], v_y)
    for copy in copies:
        copy.wait()
    coef = [coef_x[0].astype(jnp.float32), coef_x[1].astype(jnp.float32)]
    coef += [coef_y[side].astype(jnp.float32)[:, j, :] for side, j in enumerate((0, TILE - 1))]
    th = [th_x[0], th_x[1], th_y[0, :, 0, :], th_y[1, :, TILE - 1, :]]
    first_x, last_x, first_y, last_y = [-courant * (a * b) for a, b in zip(coef, th)]
    put_edges(u_x[...] + first_x, last_x, v_y[:, 0, :] + first_y, last_y, outs)
    coef_out[...] = jnp.concatenate(coef, axis=0)


def prepare_kernel(nx, ny, mat_ref, u_ref, v_ref, th_ref, coef_ref, h_ref, g_ref, split_ref):
    nz = u_ref.shape[1]
    order = mat_ref.shape[0]
    high, low = split(mat_ref[...].T)
    split_ref[:order] = high
    split_ref[order : 2 * order] = high
    split_ref[2 * order :] = low
    zero = jnp.zeros((1, nz), jnp.float32)
    for i in range(nx):
        here = pl.ds(i * ny, ny)
        v = v_ref[here, :]
        h = after(v, zero) - v - u_ref[here, :]
        if i + 1 < nx:
            h = h + u_ref[pl.ds((i + 1) * ny, ny), :]
        h_ref[here, :] = h
        g_ref[here, :] = -courant * (coef_ref[here, :].astype(jnp.float32) * th_ref[here, :])


def edges_kernel(nx, ny, mat_ref, coef_ref, h_ref, g_ref, w_ref, th_ref, *refs):
    halo, outs = refs[:4], refs[4:]
    nz = h_ref.shape[2]
    west, east = west_of(halo), east_of(halo)
    south, north = south_of(halo), north_of(halo)

    def plane(ref, i):
        return ref[i]

    def line(ref, j):
        return ref[:, j, :]

    def lateral(mid, lo, hi):
        return before(mid, lo) + after(mid, hi) - 4.0 * mid

    def edge(ref):
        return [plane(ref, 0), plane(ref, nx - 1), line(ref, 0), line(ref, ny - 1)]

    g, h = edge(g_ref), edge(h_ref)
    inner = [plane(g_ref, 1), plane(g_ref, nx - 2), line(g_ref, 1), line(g_ref, ny - 2)]
    lows = [south[:1], south[nx - 1 :], west[:1], west[ny - 1 :]]
    highs = [north[:1], north[nx - 1 :], east[:1], east[ny - 1 :]]
    outer = [west, east, south, north]
    level_div = jnp.concatenate(
        [
            h[s] + (inner[s] + outer[s]) + lateral(g[s], lows[s], highs[s])
            for s in range(4)
        ],
        axis=0,
    )
    theta = jnp.concatenate(edge(th_ref), axis=0) - courant * level_div
    right = jnp.concatenate([jnp.concatenate(edge(w_ref), axis=0), theta], axis=1)
    solved = product(right, mat_ref)
    div = level_div + level_difference(solved[:, :nz])
    new = damping * div - courant * (coef_ref[...] * solved[:, nz:])
    a, b, c = ny, 2 * ny, 2 * ny + nx
    put_edges(new[:a], new[a:b], new[b:c], new[c:], outs)


def around(i, nx, ny, g_ref, halo):
    mid = g_ref[pl.ds(i * ny, ny), :]
    west = west_of(halo) if i == 0 else g_ref[pl.ds((i - 1) * ny, ny), :]
    east = east_of(halo) if i == nx - 1 else g_ref[pl.ds((i + 1) * ny, ny), :]
    one = pl.ds(i, 1)
    return mid, west, east, before(mid, south_of(halo, one)), after(mid, north_of(halo, one))


def solve_planes(base, nx, ny, mat_ref, g_ref, h_ref, w_ref, th_ref, halo):
    nz = h_ref.shape[1]
    rights, divs = [], []
    for i in range(base, base + ROWS):
        here = pl.ds(i * ny, ny)
        mid, west, east, south, north = around(i, nx, ny, g_ref, halo)
        h = h_ref[here, :] + (west + east) + (south + north) - 4.0 * mid
        divs.append(h)
        rights.append(
            jnp.concatenate([w_ref[here, :], th_ref[here, :] - courant * h], axis=1)
        )
    solved = product(jnp.concatenate(rights, axis=0), mat_ref)
    for k in range(ROWS):
        q = solved[k * ny : (k + 1) * ny]
        w, th = q[:, :nz], q[:, nz:]
        here = pl.ds((base + k) * ny, ny)
        yield here, divs[k], w, th, divs[k] + level_difference(w)


def block_kernel(
    nx, ny, mat_ref, coef_ref, g_ref, h_ref, w_ref, th_ref, u_ref, v_ref, rho_ref, *refs
):
    halo = refs[:4]
    g_out, h_out, w_out, th_out, u_out, v_out, rho_out = refs[4:]
    for base in range(0, nx, ROWS):
        for i in range(base, base + ROWS):
            here = pl.ds(i * ny, ny)
            mid, west, _, south, _ = around(i, nx, ny, g_ref, halo)
            u_out[here, :] = u_ref[here, :] + (mid - west)
            v_out[here, :] = v_ref[here, :] + (mid - south)
        for here, h, w, th, div in solve_planes(
            base, nx, ny, mat_ref, g_ref, h_ref, w_ref, th_ref, halo
        ):
            h_out[here, :] = h
            rho_out[here, :] = rho_ref[here, :] - courant * div
            w_out[here, :] = w
            th_out[here, :] = th
            g_out[here, :] = damping * div - courant * (coef_ref[here, :].astype(jnp.float32) * th)


def last_kernel(nx, ny, mat_ref, g_ref, h_ref, w_ref, th_ref, u_ref, v_ref, rho_ref, *refs):
    halo, outs, parts, sems = refs[:4], refs[4:9], refs[9:14], refs[14]
    rho_part, u_part, v_part, w_part, th_part = parts
    copies = []

    def send(slot, start, count):
        rows = pl.ds(start * ny, count * ny)
        copies.append(
            pltpu.make_async_copy(
                parts[slot].at[rows, :], outs[slot].at[rows, :], sems.at[len(copies)]
            )
        )
        copies[-1].start()

    half = nx // 2
    for base in (0, half):
        for i in range(base, base + half):
            here = pl.ds(i * ny, ny)
            mid, west, _, south, _ = around(i, nx, ny, g_ref, halo)
            u_part[here, :] = u_ref[here, :] + (mid - west)
            v_part[here, :] = v_ref[here, :] + (mid - south)
        send(1, base, half)
        send(2, base, half)
    for base in range(0, nx, ROWS):
        for here, _, w, th, div in solve_planes(
            base, nx, ny, mat_ref, g_ref, h_ref, w_ref, th_ref, halo
        ):
            w_part[here, :] = w
            th_part[here, :] = th
            rho_part[here, :] = rho_ref[here, :] - courant * div
        for slot in (3, 4, 0):
            send(slot, base, ROWS)
    for copy in copies:
        copy.wait()


def body(density, flux_east, flux_north, flux_up, theta_pert, sound_coef, vert_inverse):
    nx, ny, nz = density.shape
    order = 2 * nz
    f32, bf16 = jnp.float32, jnp.bfloat16
    vmem = pl.BlockSpec(memory_space=pltpu.VMEM)
    hbm = pl.BlockSpec(memory_space=pltpu.HBM)
    plane_x = jax.ShapeDtypeStruct((ny, nz), f32)
    plane_y = jax.ShapeDtypeStruct((nx, nz), f32)
    planes = (plane_y, plane_x, plane_x, plane_y)
    field = jax.ShapeDtypeStruct((nx * ny, nz), f32)
    edge_columns = 2 * (nx + ny)

    def call(kernel, name, columns, limit=16, **options):
        return pl.pallas_call(
            lambda *refs: kernel(nx, ny, *refs),
            compiler_params=pltpu.CompilerParams(vmem_limit_bytes=limit * MIB),
            cost_estimate=pl.CostEstimate(
                flops=6 * columns * order * order,
                bytes_accessed=columns * nz * 4,
                transcendentals=0,
            ),
            name=name,
            **options,
        )

    def swapped(sends):
        return tuple(paired(block, *route) for block, route in zip(sends, ROUTES))

    *sends, coef_edges = call(
        first_edges_kernel,
        "first_edges",
        edge_columns,
        in_specs=[hbm] * 4,
        out_specs=[vmem] * 5,
        out_shape=planes + (jax.ShapeDtypeStruct((edge_columns, nz), f32),),
        scratch_shapes=[
            pltpu.VMEM((2, ny, nz), f32),
            pltpu.VMEM((2, nx, TILE, nz), f32),
            pltpu.VMEM((2, ny, nz), bf16),
            pltpu.VMEM((2, nx, TILE, nz), bf16),
            pltpu.VMEM((ny, nz), f32),
            pltpu.VMEM((nx, TILE, nz), f32),
            pltpu.SemaphoreType.DMA((10,)),
        ],
    )(
        *(
            pltpu.with_memory_space_constraint(array, pltpu.HBM)
            for array in (theta_pert, sound_coef, flux_east, flux_north)
        )
    )
    arrays = (flux_east, flux_north, flux_up, theta_pert, density, sound_coef)
    flat = tuple(array.reshape(nx * ny, nz) for array in arrays)
    sends, flat, vert_inverse = lax.optimization_barrier((sends, flat, vert_inverse))
    u, v, w, th, rho, coef = flat
    halo = swapped(sends)
    h, g, mat = call(
        prepare_kernel,
        "prepare",
        nx * ny,
        in_specs=[vmem] * 5,
        out_specs=[vmem] * 3,
        out_shape=(field, field, jax.ShapeDtypeStruct((3 * order, order), bf16)),
    )(vert_inverse, u, v, th, coef)
    for _ in range(SUBSTEPS - 1):
        sends = call(
            edges_kernel,
            "edges",
            edge_columns,
            in_specs=[vmem] * 10,
            out_specs=[vmem] * 4,
            out_shape=planes,
        )(mat, coef_edges, *(array.reshape(nx, ny, nz) for array in (h, g, w, th)), *halo)
        arrived = swapped(sends)
        g, h, w, th, u, v, rho = call(
            block_kernel,
            "block",
            nx * ny,
            in_specs=[vmem] * 13,
            out_specs=[vmem] * 7,
            out_shape=(field,) * 7,
        )(mat, coef, g, h, w, th, u, v, rho, *halo)
        halo = arrived
    outs = call(
        last_kernel,
        "last",
        nx * ny,
        limit=24,
        in_specs=[vmem] * 12,
        out_specs=[hbm] * 5,
        out_shape=(field,) * 5,
        scratch_shapes=[pltpu.VMEM((nx * ny, nz), f32)] * 5
        + [pltpu.SemaphoreType.DMA((4 + 3 * (nx // ROWS),))],
    )(mat, g, h, w, th, u, v, rho, *halo)
    return tuple(out.reshape(nx, ny, nz) for out in outs)


def solution(mesh):
    spec = P("gx", "gy", None)
    return jax.shard_map(
        body, mesh=mesh, in_specs=(spec,) * 6 + (P(),), out_specs=(spec,) * 5, check_vma=False
    )
```

profile of v0, /device:TPU:0, one launch (start us, length us, event | category | flops | bytes accessed | tf_op | source)
XLA Modules:
  0.0 52.4 jit_solution(9412421307619909017)
XLA Ops:
  0.7 1.7 %first_edges.1 = (f32[32,256]{1,0:T(8,128)S(1)}, f32[32,256]{1,0:T(8,128)S(1)}, f32[32,256]{1,0:T(8,128)S(1)}, f32[32,256]{1,0:T(8,128)S(1)}, f32[128,256]{1,0:T(8,128)S(1)}) custom-call(f32[32,32,256]{2,1,0:T(8,128)} %refs_0_.1, bf16[32,32,256]{2,1,0:T(8,128)(2,1)} %refs_1_.1, f32[32,32,256]{2,1,0:T(8,128)} %refs_2_.1, f32[32,32,256]{2,1,0:T(8,128)} %refs_3_.1), custom_call_target="tpu_custom_call" | custom-call | flops 201326592 | bytes 131072 | tf_op jit(solution)/shard_map/first_edges/pallas_call | solution.py:282
  2.4 4.6 %collective-permute-start = (f32[32,256]{1,0:T(8,128)S(1)}, f32[32,256]{1,0:T(8,128)S(1)}, u32[]{:S(2)}, u32[]{:S(2)}) collective-permute-start(f32[32,256]{1,0:T(8,128)S(1)} %get-tuple-element.98), channel_id=1, source_target_pairs={{1,2},{2,1},{3,4},{4,3},{5,6},{6,5},{7,0},{0,7},{9,10},{10,9},{11,... | collective-permute-start | bytes 98312 | tf_op jit(solution)/shard_map/ppermute | solution.py:26
  7.0 2.4 %collective-permute-start.1 = (f32[32,256]{1,0:T(8,128)S(1)}, f32[32,256]{1,0:T(8,128)S(1)}, u32[]{:S(2)}, u32[]{:S(2)}) collective-permute-start(f32[32,256]{1,0:T(8,128)S(1)} %get-tuple-element.99), channel_id=1, source_target_pairs={{8,16},{16,8},{24,0},{0,24},{9,17},{17,9},{25,1},{1,25},{10,18},{1... | collective-permute-start | bytes 98312 | tf_op jit(solution)/shard_map/ppermute | solution.py:26
  10.0 1.2 %copy-done.6 = f32[512,512]{1,0:T(8,128)S(1)} copy-done((f32[512,512]{1,0:T(8,128)S(1)}, f32[512,512]{1,0:T(8,128)}, u32[]{:S(2)}) %copy-start.6) | copy-done | bytes 1048600
  11.9 1.5 %collective-permute-done.2.refs_11_.refs_8_ = f32[32,256]{1,0:T(8,128)S(1)} collective-permute-done((f32[32,256]{1,0:T(8,128)S(1)}, f32[32,256]{1,0:T(8,128)S(1)}, u32[]{:S(2)}, u32[]{:S(2)}) %collective-permute-start.2) | collective-permute-done | bytes 32800 | tf_op jit(solution)/shard_map/ppermute | solution.py:26
  14.1 1.2 %collective-permute-start.5 = (f32[32,256]{1,0:T(8,128)S(1)}, f32[32,256]{1,0:T(8,128)S(1)}, u32[]{:S(2)}, u32[]{:S(2)}) collective-permute-start(f32[32,256]{1,0:T(8,128)S(1)} %get-tuple-element.111), channel_id=1, source_target_pairs={{8,16},{16,8},{24,0},{0,24},{9,17},{17,9},{25,1},{1,25},{10,18},{1... | collective-permute-start | bytes 98312 | tf_op jit(solution)/shard_map/ppermute | solution.py:26
  15.3 0.8 %collective-permute-start.6 = (f32[32,256]{1,0:T(8,128)S(1)}, f32[32,256]{1,0:T(8,128)S(1)}, u32[]{:S(2)}, u32[]{:S(2)}) collective-permute-start(f32[32,256]{1,0:T(8,128)S(1)} %get-tuple-element.112), channel_id=1, source_target_pairs={{0,8},{8,0},{16,24},{24,16},{1,9},{9,1},{17,25},{25,17},{2,10},{10... | collective-permute-start | bytes 98312 | tf_op jit(solution)/shard_map/ppermute | solution.py:26
  16.1 2.4 %block.5 = (f32[1024,256]{1,0:T(8,128)S(1)}, f32[1024,256]{1,0:T(8,128)S(1)}, f32[1024,256]{1,0:T(8,128)S(1)}, f32[1024,256]{1,0:T(8,128)S(1)}, f32[1024,256]{1,...) custom-call(bf16[1536,512]{1,0:T(8,128)(2,1)S(1)} %get-tuple-element.93.refs_0_, ...), custom_call_target="tpu_custom_call" | custom-call | flops 1610612736 | bytes 1048576 | tf_op jit(solution)/shard_map/block/pallas_call | solution.py:327
  18.5 0.7 %collective-permute-done.4.refs_9_.refs_6_ = f32[32,256]{1,0:T(8,128)S(1)} collective-permute-done((f32[32,256]{1,0:T(8,128)S(1)}, f32[32,256]{1,0:T(8,128)S(1)}, u32[]{:S(2)}, u32[]{:S(2)}) %collective-permute-start.4) | collective-permute-done | bytes 32800 | tf_op jit(solution)/shard_map/ppermute | solution.py:26
  19.9 2.3 %collective-permute-start.8 = (f32[32,256]{1,0:T(8,128)S(1)}, f32[32,256]{1,0:T(8,128)S(1)}, u32[]{:S(2)}, u32[]{:S(2)}) collective-permute-start(f32[32,256]{1,0:T(8,128)S(1)} %get-tuple-element.121), channel_id=1, source_target_pairs={{1,2},{2,1},{3,4},{4,3},{5,6},{6,5},{7,0},{0,7},{9,10},{10,9},{11,... | collective-permute-start | bytes 98312 | tf_op jit(solution)/shard_map/ppermute | solution.py:26
  22.2 1.6 %collective-permute-start.9 = (f32[32,256]{1,0:T(8,128)S(1)}, f32[32,256]{1,0:T(8,128)S(1)}, u32[]{:S(2)}, u32[]{:S(2)}) collective-permute-start(f32[32,256]{1,0:T(8,128)S(1)} %get-tuple-element.122), channel_id=1, source_target_pairs={{8,16},{16,8},{24,0},{0,24},{9,17},{17,9},{25,1},{1,25},{10,18},{1... | collective-permute-start | bytes 98312 | tf_op jit(solution)/shard_map/ppermute | solution.py:26
  23.8 1.4 %collective-permute-start.10 = (f32[32,256]{1,0:T(8,128)S(1)}, f32[32,256]{1,0:T(8,128)S(1)}, u32[]{:S(2)}, u32[]{:S(2)}) collective-permute-start(f32[32,256]{1,0:T(8,128)S(1)} %get-tuple-element.123), channel_id=1, source_target_pairs={{0,8},{8,0},{16,24},{24,16},{1,9},{9,1},{17,25},{25,17},{2,10},{10... | collective-permute-start | bytes 98312 | tf_op jit(solution)/shard_map/ppermute | solution.py:26
  25.2 2.4 %block.6 = (f32[1024,256]{1,0:T(8,128)S(1)}, f32[1024,256]{1,0:T(8,128)S(1)}, f32[1024,256]{1,0:T(8,128)S(1)}, f32[1024,256]{1,0:T(8,128)S(1)}, f32[1024,256]{1,...) custom-call(bf16[1536,512]{1,0:T(8,128)(2,1)S(1)} %get-tuple-element.93.refs_0_, ...), custom_call_target="tpu_custom_call" | custom-call | flops 1610612736 | bytes 1048576 | tf_op jit(solution)/shard_map/block/pallas_call | solution.py:327
  28.9 1.4 %collective-permute-start.13 = (f32[32,256]{1,0:T(8,128)S(1)}, f32[32,256]{1,0:T(8,128)S(1)}, u32[]{:S(2)}, u32[]{:S(2)}) collective-permute-start(f32[32,256]{1,0:T(8,128)S(1)} %get-tuple-element.133), channel_id=1, source_target_pairs={{8,16},{16,8},{24,0},{0,24},{9,17},{17,9},{25,1},{1,25},{10,18},{1... | collective-permute-start | bytes 98312 | tf_op jit(solution)/shard_map/ppermute | solution.py:26
  30.3 0.8 %collective-permute-start.14 = (f32[32,256]{1,0:T(8,128)S(1)}, f32[32,256]{1,0:T(8,128)S(1)}, u32[]{:S(2)}, u32[]{:S(2)}) collective-permute-start(f32[32,256]{1,0:T(8,128)S(1)} %get-tuple-element.134), channel_id=1, source_target_pairs={{0,8},{8,0},{16,24},{24,16},{1,9},{9,1},{17,25},{25,17},{2,10},{10... | collective-permute-start | bytes 98312 | tf_op jit(solution)/shard_map/ppermute | solution.py:26
  31.0 2.4 %block.7 = (f32[1024,256]{1,0:T(8,128)S(1)}, f32[1024,256]{1,0:T(8,128)S(1)}, f32[1024,256]{1,0:T(8,128)S(1)}, f32[1024,256]{1,0:T(8,128)S(1)}, f32[1024,256]{1,...) custom-call(bf16[1536,512]{1,0:T(8,128)(2,1)S(1)} %get-tuple-element.93.refs_0_, ...), custom_call_target="tpu_custom_call" | custom-call | flops 1610612736 | bytes 1048576 | tf_op jit(solution)/shard_map/block/pallas_call | solution.py:327
  34.8 2.0 %collective-permute-start.16 = (f32[32,256]{1,0:T(8,128)S(1)}, f32[32,256]{1,0:T(8,128)S(1)}, u32[]{:S(2)}, u32[]{:S(2)}) collective-permute-start(f32[32,256]{1,0:T(8,128)S(1)} %get-tuple-element.143), channel_id=1, source_target_pairs={{1,2},{2,1},{3,4},{4,3},{5,6},{6,5},{7,0},{0,7},{9,10},{10,9},{11,... | collective-permute-start | bytes 98312 | tf_op jit(solution)/shard_map/ppermute | solution.py:26
  36.8 2.0 %collective-permute-start.17 = (f32[32,256]{1,0:T(8,128)S(1)}, f32[32,256]{1,0:T(8,128)S(1)}, u32[]{:S(2)}, u32[]{:S(2)}) collective-permute-start(f32[32,256]{1,0:T(8,128)S(1)} %get-tuple-element.144), channel_id=1, source_target_pairs={{8,16},{16,8},{24,0},{0,24},{9,17},{17,9},{25,1},{1,25},{10,18},{1... | collective-permute-start | bytes 98312 | tf_op jit(solution)/shard_map/ppermute | solution.py:26
  39.5 2.6 %block.8 = (f32[1024,256]{1,0:T(8,128)S(1)}, f32[1024,256]{1,0:T(8,128)S(1)}, f32[1024,256]{1,0:T(8,128)S(1)}, f32[1024,256]{1,0:T(8,128)S(1)}, f32[1024,256]{1,...) custom-call(bf16[1536,512]{1,0:T(8,128)(2,1)S(1)} %get-tuple-element.93.refs_0_, ...), custom_call_target="tpu_custom_call" | custom-call | flops 1610612736 | bytes 1048576 | tf_op jit(solution)/shard_map/block/pallas_call | solution.py:327
  42.1 0.7 %collective-permute-done.18.refs_11_.refs_8_ = f32[32,256]{1,0:T(8,128)S(1)} collective-permute-done((f32[32,256]{1,0:T(8,128)S(1)}, f32[32,256]{1,0:T(8,128)S(1)}, u32[]{:S(2)}, u32[]{:S(2)}) %collective-permute-start.18) | collective-permute-done | bytes 32800 | tf_op jit(solution)/shard_map/ppermute | solution.py:26
  43.7 1.2 %collective-permute-start.21 = (f32[32,256]{1,0:T(8,128)S(1)}, f32[32,256]{1,0:T(8,128)S(1)}, u32[]{:S(2)}, u32[]{:S(2)}) collective-permute-start(f32[32,256]{1,0:T(8,128)S(1)} %get-tuple-element.155), channel_id=1, source_target_pairs={{8,16},{16,8},{24,0},{0,24},{9,17},{17,9},{25,1},{1,25},{10,18},{1... | collective-permute-start | bytes 98312 | tf_op jit(solution)/shard_map/ppermute | solution.py:26
  44.9 1.3 %collective-permute-start.22 = (f32[32,256]{1,0:T(8,128)S(1)}, f32[32,256]{1,0:T(8,128)S(1)}, u32[]{:S(2)}, u32[]{:S(2)}) collective-permute-start(f32[32,256]{1,0:T(8,128)S(1)} %get-tuple-element.156), channel_id=1, source_target_pairs={{0,8},{8,0},{16,24},{24,16},{1,9},{9,1},{17,25},{25,17},{2,10},{10... | collective-permute-start | bytes 98312 | tf_op jit(solution)/shard_map/ppermute | solution.py:26
  46.2 2.4 %block.9 = (f32[1024,256]{1,0:T(8,128)S(1)}, f32[1024,256]{1,0:T(8,128)S(1)}, f32[1024,256]{1,0:T(8,128)S(1)}, f32[1024,256]{1,0:T(8,128)S(1)}, f32[1024,256]{1,...) custom-call(bf16[1536,512]{1,0:T(8,128)(2,1)S(1)} %get-tuple-element.93.refs_0_, ...), custom_call_target="tpu_custom_call" | custom-call | flops 1610612736 | bytes 1048576 | tf_op jit(solution)/shard_map/block/pallas_call | solution.py:327
  48.8 3.5 %last.1 = (f32[1024,256]{1,0:T(8,128)}, f32[1024,256]{1,0:T(8,128)}, f32[1024,256]{1,0:T(8,128)}, f32[1024,256]{1,0:T(8,128)}, f32[1024,256]{1,0:T(8,128)}) custom-call(bf16[1536,512]{1,0:T(8,128)(2,1)S(1)} %get-tuple-element.93.refs_0_, f32[1024,256]{1,0:T(8,128)S(1)} %get-tuple-element.147.refs_1_, f32[1024,256]{1,0:T(8,128)S(1)} %get-tuple-element.148.refs_2_, ...), custom_call_target="tpu_custom_call" | custom-call | flops 1610612736 | bytes 1048576 | tf_op jit(solution)/shard_map/last/pallas_call | solution.py:336
  (51 shorter events, 7.2 us)
Async XLA Ops:
  2.4 9.4 %collective-permute-start = (f32[32,256]{1,0:T(8,128)S(1)}, f32[32,256]{1,0:T(8,128)S(1)}, u32[]{:S(2)}, u32[]{:S(2)}) collective-permute-start(f32[32,256]{1,0:T(8,128)S(1)} %get-tuple-element.98), channel_id=1, source_target_pairs={{1,2},{2,1},{3,4},{4,3},{5,6},{6,5},{7,0},{0,7},{9,10},{10,9},{11,... | collective-permute-start | bytes 98312 | tf_op jit(solution)/shard_map/ppermute | solution.py:26
  7.0 4.9 %collective-permute-start.1 = (f32[32,256]{1,0:T(8,128)S(1)}, f32[32,256]{1,0:T(8,128)S(1)}, u32[]{:S(2)}, u32[]{:S(2)}) collective-permute-start(f32[32,256]{1,0:T(8,128)S(1)} %get-tuple-element.99), channel_id=1, source_target_pairs={{8,16},{16,8},{24,0},{0,24},{9,17},{17,9},{25,1},{1,25},{10,18},{1... | collective-permute-start | bytes 98312 | tf_op jit(solution)/shard_map/ppermute | solution.py:26
  9.5 3.9 %collective-permute-start.2 = (f32[32,256]{1,0:T(8,128)S(1)}, f32[32,256]{1,0:T(8,128)S(1)}, u32[]{:S(2)}, u32[]{:S(2)}) collective-permute-start(f32[32,256]{1,0:T(8,128)S(1)} %get-tuple-element.100), channel_id=1, source_target_pairs={{0,8},{8,0},{16,24},{24,16},{1,9},{9,1},{17,25},{25,17},{2,10},{10... | collective-permute-start | bytes 98312 | tf_op jit(solution)/shard_map/ppermute | solution.py:26
  10.0 3.4 %collective-permute-start.3 = (f32[32,256]{1,0:T(8,128)S(1)}, f32[32,256]{1,0:T(8,128)S(1)}, u32[]{:S(2)}, u32[]{:S(2)}) collective-permute-start(f32[32,256]{1,0:T(8,128)S(1)} %get-tuple-element.101), channel_id=1, source_target_pairs={{0,1},{1,0},{2,3},{3,2},{4,5},{5,4},{6,7},{7,6},{8,9},{9,8},{10,11... | collective-permute-start | bytes 98312 | tf_op jit(solution)/shard_map/ppermute | solution.py:26
  14.0 5.2 %collective-permute-start.4 = (f32[32,256]{1,0:T(8,128)S(1)}, f32[32,256]{1,0:T(8,128)S(1)}, u32[]{:S(2)}, u32[]{:S(2)}) collective-permute-start(f32[32,256]{1,0:T(8,128)S(1)} %get-tuple-element.110), channel_id=1, source_target_pairs={{1,2},{2,1},{3,4},{4,3},{5,6},{6,5},{7,0},{0,7},{9,10},{10,9},{11,... | collective-permute-start | bytes 98312 | tf_op jit(solution)/shard_map/ppermute | solution.py:26
  14.1 5.1 %collective-permute-start.5 = (f32[32,256]{1,0:T(8,128)S(1)}, f32[32,256]{1,0:T(8,128)S(1)}, u32[]{:S(2)}, u32[]{:S(2)}) collective-permute-start(f32[32,256]{1,0:T(8,128)S(1)} %get-tuple-element.111), channel_id=1, source_target_pairs={{8,16},{16,8},{24,0},{0,24},{9,17},{17,9},{25,1},{1,25},{10,18},{1... | collective-permute-start | bytes 98312 | tf_op jit(solution)/shard_map/ppermute | solution.py:26
  15.3 3.9 %collective-permute-start.6 = (f32[32,256]{1,0:T(8,128)S(1)}, f32[32,256]{1,0:T(8,128)S(1)}, u32[]{:S(2)}, u32[]{:S(2)}) collective-permute-start(f32[32,256]{1,0:T(8,128)S(1)} %get-tuple-element.112), channel_id=1, source_target_pairs={{0,8},{8,0},{16,24},{24,16},{1,9},{9,1},{17,25},{25,17},{2,10},{10... | collective-permute-start | bytes 98312 | tf_op jit(solution)/shard_map/ppermute | solution.py:26
  16.1 3.1 %collective-permute-start.7 = (f32[32,256]{1,0:T(8,128)S(1)}, f32[32,256]{1,0:T(8,128)S(1)}, u32[]{:S(2)}, u32[]{:S(2)}) collective-permute-start(f32[32,256]{1,0:T(8,128)S(1)} %get-tuple-element.113), channel_id=1, source_target_pairs={{0,1},{1,0},{2,3},{3,2},{4,5},{5,4},{6,7},{7,6},{8,9},{9,8},{10,11... | collective-permute-start | bytes 98312 | tf_op jit(solution)/shard_map/ppermute | solution.py:26
  19.9 7.6 %collective-permute-start.8 = (f32[32,256]{1,0:T(8,128)S(1)}, f32[32,256]{1,0:T(8,128)S(1)}, u32[]{:S(2)}, u32[]{:S(2)}) collective-permute-start(f32[32,256]{1,0:T(8,128)S(1)} %get-tuple-element.121), channel_id=1, source_target_pairs={{1,2},{2,1},{3,4},{4,3},{5,6},{6,5},{7,0},{0,7},{9,10},{10,9},{11,... | collective-permute-start | bytes 98312 | tf_op jit(solution)/shard_map/ppermute | solution.py:26
  22.2 5.4 %collective-permute-start.9 = (f32[32,256]{1,0:T(8,128)S(1)}, f32[32,256]{1,0:T(8,128)S(1)}, u32[]{:S(2)}, u32[]{:S(2)}) collective-permute-start(f32[32,256]{1,0:T(8,128)S(1)} %get-tuple-element.122), channel_id=1, source_target_pairs={{8,16},{16,8},{24,0},{0,24},{9,17},{17,9},{25,1},{1,25},{10,18},{1... | collective-permute-start | bytes 98312 | tf_op jit(solution)/shard_map/ppermute | solution.py:26
  23.8 3.9 %collective-permute-start.10 = (f32[32,256]{1,0:T(8,128)S(1)}, f32[32,256]{1,0:T(8,128)S(1)}, u32[]{:S(2)}, u32[]{:S(2)}) collective-permute-start(f32[32,256]{1,0:T(8,128)S(1)} %get-tuple-element.123), channel_id=1, source_target_pairs={{0,8},{8,0},{16,24},{24,16},{1,9},{9,1},{17,25},{25,17},{2,10},{10... | collective-permute-start | bytes 98312 | tf_op jit(solution)/shard_map/ppermute | solution.py:26
  25.2 2.5 %collective-permute-start.11 = (f32[32,256]{1,0:T(8,128)S(1)}, f32[32,256]{1,0:T(8,128)S(1)}, u32[]{:S(2)}, u32[]{:S(2)}) collective-permute-start(f32[32,256]{1,0:T(8,128)S(1)} %get-tuple-element.124), channel_id=1, source_target_pairs={{0,1},{1,0},{2,3},{3,2},{4,5},{5,4},{6,7},{7,6},{8,9},{9,8},{10,11... | collective-permute-start | bytes 98312 | tf_op jit(solution)/shard_map/ppermute | solution.py:26
  28.3 5.2 %collective-permute-start.12 = (f32[32,256]{1,0:T(8,128)S(1)}, f32[32,256]{1,0:T(8,128)S(1)}, u32[]{:S(2)}, u32[]{:S(2)}) collective-permute-start(f32[32,256]{1,0:T(8,128)S(1)} %get-tuple-element.132), channel_id=1, source_target_pairs={{1,2},{2,1},{3,4},{4,3},{5,6},{6,5},{7,0},{0,7},{9,10},{10,9},{11,... | collective-permute-start | bytes 98312 | tf_op jit(solution)/shard_map/ppermute | solution.py:26
  28.9 4.8 %collective-permute-start.13 = (f32[32,256]{1,0:T(8,128)S(1)}, f32[32,256]{1,0:T(8,128)S(1)}, u32[]{:S(2)}, u32[]{:S(2)}) collective-permute-start(f32[32,256]{1,0:T(8,128)S(1)} %get-tuple-element.133), channel_id=1, source_target_pairs={{8,16},{16,8},{24,0},{0,24},{9,17},{17,9},{25,1},{1,25},{10,18},{1... | collective-permute-start | bytes 98312 | tf_op jit(solution)/shard_map/ppermute | solution.py:26
  30.3 3.9 %collective-permute-start.14 = (f32[32,256]{1,0:T(8,128)S(1)}, f32[32,256]{1,0:T(8,128)S(1)}, u32[]{:S(2)}, u32[]{:S(2)}) collective-permute-start(f32[32,256]{1,0:T(8,128)S(1)} %get-tuple-element.134), channel_id=1, source_target_pairs={{0,8},{8,0},{16,24},{24,16},{1,9},{9,1},{17,25},{25,17},{2,10},{10... | collective-permute-start | bytes 98312 | tf_op jit(solution)/shard_map/ppermute | solution.py:26
  31.0 3.2 %collective-permute-start.15 = (f32[32,256]{1,0:T(8,128)S(1)}, f32[32,256]{1,0:T(8,128)S(1)}, u32[]{:S(2)}, u32[]{:S(2)}) collective-permute-start(f32[32,256]{1,0:T(8,128)S(1)} %get-tuple-element.135), channel_id=1, source_target_pairs={{0,1},{1,0},{2,3},{3,2},{4,5},{5,4},{6,7},{7,6},{8,9},{9,8},{10,11... | collective-permute-start | bytes 98312 | tf_op jit(solution)/shard_map/ppermute | solution.py:26
  34.8 7.2 %collective-permute-start.16 = (f32[32,256]{1,0:T(8,128)S(1)}, f32[32,256]{1,0:T(8,128)S(1)}, u32[]{:S(2)}, u32[]{:S(2)}) collective-permute-start(f32[32,256]{1,0:T(8,128)S(1)} %get-tuple-element.143), channel_id=1, source_target_pairs={{1,2},{2,1},{3,4},{4,3},{5,6},{6,5},{7,0},{0,7},{9,10},{10,9},{11,... | collective-permute-start | bytes 98312 | tf_op jit(solution)/shard_map/ppermute | solution.py:26
  36.8 5.2 %collective-permute-start.17 = (f32[32,256]{1,0:T(8,128)S(1)}, f32[32,256]{1,0:T(8,128)S(1)}, u32[]{:S(2)}, u32[]{:S(2)}) collective-permute-start(f32[32,256]{1,0:T(8,128)S(1)} %get-tuple-element.144), channel_id=1, source_target_pairs={{8,16},{16,8},{24,0},{0,24},{9,17},{17,9},{25,1},{1,25},{10,18},{1... | collective-permute-start | bytes 98312 | tf_op jit(solution)/shard_map/ppermute | solution.py:26
  38.8 3.9 %collective-permute-start.18 = (f32[32,256]{1,0:T(8,128)S(1)}, f32[32,256]{1,0:T(8,128)S(1)}, u32[]{:S(2)}, u32[]{:S(2)}) collective-permute-start(f32[32,256]{1,0:T(8,128)S(1)} %get-tuple-element.145), channel_id=1, source_target_pairs={{0,8},{8,0},{16,24},{24,16},{1,9},{9,1},{17,25},{25,17},{2,10},{10... | collective-permute-start | bytes 98312 | tf_op jit(solution)/shard_map/ppermute | solution.py:26
  39.5 3.3 %collective-permute-start.19 = (f32[32,256]{1,0:T(8,128)S(1)}, f32[32,256]{1,0:T(8,128)S(1)}, u32[]{:S(2)}, u32[]{:S(2)}) collective-permute-start(f32[32,256]{1,0:T(8,128)S(1)} %get-tuple-element.146), channel_id=1, source_target_pairs={{0,1},{1,0},{2,3},{3,2},{4,5},{5,4},{6,7},{7,6},{8,9},{9,8},{10,11... | collective-permute-start | bytes 98312 | tf_op jit(solution)/shard_map/ppermute | solution.py:26
  43.4 5.2 %collective-permute-start.20 = (f32[32,256]{1,0:T(8,128)S(1)}, f32[32,256]{1,0:T(8,128)S(1)}, u32[]{:S(2)}, u32[]{:S(2)}) collective-permute-start(f32[32,256]{1,0:T(8,128)S(1)} %get-tuple-element.154), channel_id=1, source_target_pairs={{1,2},{2,1},{3,4},{4,3},{5,6},{6,5},{7,0},{0,7},{9,10},{10,9},{11,... | collective-permute-start | bytes 98312 | tf_op jit(solution)/shard_map/ppermute | solution.py:26
  43.7 5.0 %collective-permute-start.21 = (f32[32,256]{1,0:T(8,128)S(1)}, f32[32,256]{1,0:T(8,128)S(1)}, u32[]{:S(2)}, u32[]{:S(2)}) collective-permute-start(f32[32,256]{1,0:T(8,128)S(1)} %get-tuple-element.155), channel_id=1, source_target_pairs={{8,16},{16,8},{24,0},{0,24},{9,17},{17,9},{25,1},{1,25},{10,18},{1... | collective-permute-start | bytes 98312 | tf_op jit(solution)/shard_map/ppermute | solution.py:26
  44.9 3.9 %collective-permute-start.22 = (f32[32,256]{1,0:T(8,128)S(1)}, f32[32,256]{1,0:T(8,128)S(1)}, u32[]{:S(2)}, u32[]{:S(2)}) collective-permute-start(f32[32,256]{1,0:T(8,128)S(1)} %get-tuple-element.156), channel_id=1, source_target_pairs={{0,8},{8,0},{16,24},{24,16},{1,9},{9,1},{17,25},{25,17},{2,10},{10... | collective-permute-start | bytes 98312 | tf_op jit(solution)/shard_map/ppermute | solution.py:26
  46.2 2.7 %collective-permute-start.23 = (f32[32,256]{1,0:T(8,128)S(1)}, f32[32,256]{1,0:T(8,128)S(1)}, u32[]{:S(2)}, u32[]{:S(2)}) collective-permute-start(f32[32,256]{1,0:T(8,128)S(1)} %get-tuple-element.157), channel_id=1, source_target_pairs={{0,1},{1,0},{2,3},{3,2},{4,5},{5,4},{6,7},{7,6},{8,9},{9,8},{10,11... | collective-permute-start | bytes 98312 | tf_op jit(solution)/shard_map/ppermute | solution.py:26
  (7 other events, 52.4 us)
where the time goes:
time: 52.6 us; the launch traced here: 52.4 us
  starting transfers between devices  25.1 us (48%)
  Pallas kernels  21 us (40%)
  waiting for transfers between devices  4.1 us (8%)
  local copies, waits for them, and re-layouts  1.25 us (2%)
  between operations  1.04 us (2%)
    ppermute x24, starting transfers between devices, paired(): return lax.ppermute(block, axis, route)  25.1 us
    pallas_call x5, Pallas kernels, body(): call(block_kernel, 'block', nx * ny, in_specs=[vmem] * 13, out_specs=[vme...  12 us
    ppermute x24, waiting for transfers between devices, paired(): return lax.ppermute(block, axis, route)  4.1 us
    pallas_call x1, Pallas kernels, body(): call(last_kernel, 'last', nx * ny, limit=24, in_specs=[vmem] * 12, out_sp...  3.45 us
    pallas_call x5, Pallas kernels, body(): call(edges_kernel, 'edges', edge_columns, in_specs=[vmem] * 10, out_specs...  3.16 us
    pallas_call x1, Pallas kernels, body(): call(first_edges_kernel, 'first_edges', edge_columns, in_specs=[hbm] * 4,...  1.74 us
    unnamed x14, local copies, waits for them, and re-layouts  1.25 us
  transfers between devices with their start and end apart: 24, of which 10 were waited for; matrix products, arithmetic and copies ran while one was open for 0% of the time, Pallas kernels for 24%

commit v1 on v0

--- a/solution.py
+++ b/solution.py
@@ -1,3 +1,5 @@
+import functools
+
 import jax
 import jax.numpy as jnp
 from jax import lax
@@ -63,9 +65,12 @@
     return high, low
 
 
-def product(value, mat_ref):
-    high, low = split(value)
-    terms = jnp.concatenate([high, low, high], axis=1)
+def product(upward, theta, mat_ref):
+    terms = []
+    for value in (upward, theta):
+        high, low = split(value)
+        terms += [high, low, high]
+    terms = jnp.concatenate(terms, axis=1)
     return jnp.dot(terms, mat_ref[...], preferred_element_type=jnp.float32)
 
 
@@ -97,26 +102,42 @@
         fetch(coef_hbm.at[i], coef_x.at[side])
     fetch(u_hbm.at[0], u_x)
     for side, j in enumerate((0, ny - TILE)):
-        fetch(th_hbm.at[:, pl.ds(j, TILE), :], th_y.at[side])
         fetch(coef_hbm.at[:, pl.ds(j, TILE), :], coef_y.at[side])
-    fetch(v_hbm.at[:, pl.ds(0, TILE), :], v_y)
+    for side, j in enumerate((0, ny - 1)):
+        fetch(th_hbm.at[:, j, :], th_y.at[side])
+    fetch(v_hbm.at[:, 0, :], v_y)
     for copy in copies:
         copy.wait()
     coef = [coef_x[0].astype(jnp.float32), coef_x[1].astype(jnp.float32)]
     coef += [coef_y[side].astype(jnp.float32)[:, j, :] for side, j in enumerate((0, TILE - 1))]
-    th = [th_x[0], th_x[1], th_y[0, :, 0, :], th_y[1, :, TILE - 1, :]]
+    th = [th_x[0], th_x[1], th_y[0], th_y[1]]
     first_x, last_x, first_y, last_y = [-courant * (a * b) for a, b in zip(coef, th)]
-    put_edges(u_x[...] + first_x, last_x, v_y[:, 0, :] + first_y, last_y, outs)
+    put_edges(u_x[...] + first_x, last_x, v_y[...] + first_y, last_y, outs)
     coef_out[...] = jnp.concatenate(coef, axis=0)
 
 
-def prepare_kernel(nx, ny, mat_ref, u_ref, v_ref, th_ref, coef_ref, h_ref, g_ref, split_ref):
+def prepare_kernel(nx, ny, mat_hbm, u_hbm, v_hbm, th_hbm, coef_hbm, *refs):
+    h_ref, g_ref, split_ref, u_ref, v_ref, th_ref, coef_ref, mat_ref, sems = refs
     nz = u_ref.shape[1]
     order = mat_ref.shape[0]
+    pairs = (
+        (mat_hbm, mat_ref),
+        (v_hbm, v_ref),
+        (u_hbm, u_ref),
+        (coef_hbm, coef_ref),
+        (th_hbm, th_ref),
+    )
+    copies = [pltpu.make_async_copy(*pair, sems.at[k]) for k, pair in enumerate(pairs)]
+    for copy in copies:
+        copy.start()
+    copies[0].wait()
     high, low = split(mat_ref[...].T)
-    split_ref[:order] = high
-    split_ref[order : 2 * order] = high
-    split_ref[2 * order :] = low
+    for part in range(2):
+        rows = slice(part * nz, (part + 1) * nz)
+        for slot, factor in enumerate((high, high, low)):
+            split_ref[pl.ds((3 * part + slot) * nz, nz), :] = factor[rows]
+    copies[1].wait()
+    copies[2].wait()
     zero = jnp.zeros((1, nz), jnp.float32)
     for i in range(nx):
         here = pl.ds(i * ny, ny)
@@ -125,14 +146,20 @@
         if i + 1 < nx:
             h = h + u_ref[pl.ds((i + 1) * ny, ny), :]
         h_ref[here, :] = h
+    copies[3].wait()
+    copies[4].wait()
+    for i in range(nx):
+        here = pl.ds(i * ny, ny)
         g_ref[here, :] = -courant * (coef_ref[here, :].astype(jnp.float32) * th_ref[here, :])
 
 
-def edges_kernel(nx, ny, mat_ref, coef_ref, h_ref, g_ref, w_ref, th_ref, *refs):
-    halo, outs = refs[:4], refs[4:]
-    nz = h_ref.shape[2]
+def edges_kernel(packed, nx, ny, mat_ref, coef_ref, h_ref, w_ref, th_ref, edge_g_ref, g_ref, *refs):
+    halo, outs = refs[:4], refs[4:8]
+    nz = g_ref.shape[2]
     west, east = west_of(halo), east_of(halo)
     south, north = south_of(halo), north_of(halo)
+    a, b, c, d = ny, 2 * ny, 2 * ny + nx, 2 * (ny + nx)
+    bounds = ((0, a), (a, b), (b, c), (c, d))
 
     def plane(ref, i):
         return ref[i]
@@ -144,27 +171,28 @@
         return before(mid, lo) + after(mid, hi) - 4.0 * mid
 
     def edge(ref):
-        return [plane(ref, 0), plane(ref, nx - 1), line(ref, 0), line(ref, ny - 1)]
-
-    g, h = edge(g_ref), edge(h_ref)
+        if packed:
+            return ref[...]
+        parts = [plane(ref, 0), plane(ref, nx - 1), line(ref, 0), line(ref, ny - 1)]
+        return jnp.concatenate(parts, axis=0)
+
+    g = edge(edge_g_ref)
     inner = [plane(g_ref, 1), plane(g_ref, nx - 2), line(g_ref, 1), line(g_ref, ny - 2)]
     lows = [south[:1], south[nx - 1 :], west[:1], west[ny - 1 :]]
     highs = [north[:1], north[nx - 1 :], east[:1], east[ny - 1 :]]
     outer = [west, east, south, north]
-    level_div = jnp.concatenate(
-        [
-            h[s] + (inner[s] + outer[s]) + lateral(g[s], lows[s], highs[s])
-            for s in range(4)
-        ],
-        axis=0,
-    )
-    theta = jnp.concatenate(edge(th_ref), axis=0) - courant * level_div
-    right = jnp.concatenate([jnp.concatenate(edge(w_ref), axis=0), theta], axis=1)
-    solved = product(right, mat_ref)
-    div = level_div + level_difference(solved[:, :nz])
-    new = damping * div - courant * (coef_ref[...] * solved[:, nz:])
-    a, b, c = ny, 2 * ny, 2 * ny + nx
-    put_edges(new[:a], new[a:b], new[b:c], new[c:], outs)
+    change = [
+        (inner[s] + outer[s]) + lateral(g[slice(*bounds[s])], lows[s], highs[s]) for s in range(4)
+    ]
+    level_div = edge(h_ref) + jnp.concatenate(change, axis=0)
+    theta = edge(th_ref) - courant * level_div
+    solved = product(edge(w_ref), theta, mat_ref)
+    upward, theta = solved[:, :nz], solved[:, nz:]
+    div = level_div + level_difference(upward)
+    new = damping * div - courant * (coef_ref[...] * theta)
+    put_edges(*(new[slice(*bound)] for bound in bounds), outs)
+    for ref, value in zip(refs[8:], (level_div, upward, theta, new)):
+        ref[...] = value
 
 
 def around(i, nx, ny, g_ref, halo):
@@ -175,19 +203,18 @@
     return mid, west, east, before(mid, south_of(halo, one)), after(mid, north_of(halo, one))
 
 
-def solve_planes(base, nx, ny, mat_ref, g_ref, h_ref, w_ref, th_ref, halo):
+def solve_planes(base, count, nx, ny, mat_ref, g_ref, h_ref, w_ref, th_ref, halo):
     nz = h_ref.shape[1]
-    rights, divs = [], []
-    for i in range(base, base + ROWS):
+    ws, ths, divs = [], [], []
+    for i in range(base, base + count):
         here = pl.ds(i * ny, ny)
         mid, west, east, south, north = around(i, nx, ny, g_ref, halo)
         h = h_ref[here, :] + (west + east) + (south + north) - 4.0 * mid
         divs.append(h)
-        rights.append(
-            jnp.concatenate([w_ref[here, :], th_ref[here, :] - courant * h], axis=1)
-        )
-    solved = product(jnp.concatenate(rights, axis=0), mat_ref)
-    for k in range(ROWS):
+        ws.append(w_ref[here, :])
+        ths.append(th_ref[here, :] - courant * h)
+    solved = product(jnp.concatenate(ws, axis=0), jnp.concatenate(ths, axis=0), mat_ref)
+    for k in range(count):
         q = solved[k * ny : (k + 1) * ny]
         w, th = q[:, :nz], q[:, nz:]
         here = pl.ds((base + k) * ny, ny)
@@ -206,13 +233,19 @@
             u_out[here, :] = u_ref[here, :] + (mid - west)
             v_out[here, :] = v_ref[here, :] + (mid - south)
         for here, h, w, th, div in solve_planes(
-            base, nx, ny, mat_ref, g_ref, h_ref, w_ref, th_ref, halo
+            base, ROWS, nx, ny, mat_ref, g_ref, h_ref, w_ref, th_ref, halo
         ):
             h_out[here, :] = h
             rho_out[here, :] = rho_ref[here, :] - courant * div
             w_out[here, :] = w
             th_out[here, :] = th
             g_out[here, :] = damping * div - courant * (coef_ref[here, :].astype(jnp.float32) * th)
+
+
+def last_pieces(nx):
+    pieces = [(base, ROWS) for base in range(0, nx - ROWS, ROWS)]
+    half = ROWS // 2
+    return pieces + [(nx - ROWS, half), (nx - half, half)]
 
 
 def last_kernel(nx, ny, mat_ref, g_ref, h_ref, w_ref, th_ref, u_ref, v_ref, rho_ref, *refs):
@@ -229,24 +262,30 @@
         )
         copies[-1].start()
 
-    half = nx // 2
-    for base in (0, half):
-        for i in range(base, base + half):
+    def fluxes(base, count):
+        for i in range(base, base + count):
             here = pl.ds(i * ny, ny)
             mid, west, _, south, _ = around(i, nx, ny, g_ref, halo)
             u_part[here, :] = u_ref[here, :] + (mid - west)
             v_part[here, :] = v_ref[here, :] + (mid - south)
-        send(1, base, half)
-        send(2, base, half)
-    for base in range(0, nx, ROWS):
+        for slot in (1, 2):
+            send(slot, base, count)
+
+    pieces = last_pieces(nx)
+    for base, count in pieces:
+        if base == 0:
+            fluxes(base, count)
+        if base + count < nx:
+            ahead = dict(pieces)[base + count]
+            fluxes(base + count, ahead)
         for here, _, w, th, div in solve_planes(
-            base, nx, ny, mat_ref, g_ref, h_ref, w_ref, th_ref, halo
+            base, count, nx, ny, mat_ref, g_ref, h_ref, w_ref, th_ref, halo
         ):
             w_part[here, :] = w
             th_part[here, :] = th
             rho_part[here, :] = rho_ref[here, :] - courant * div
         for slot in (3, 4, 0):
-            send(slot, base, ROWS)
+            send(slot, base, count)
     for copy in copies:
         copy.wait()
 
@@ -288,11 +327,11 @@
         out_shape=planes + (jax.ShapeDtypeStruct((edge_columns, nz), f32),),
         scratch_shapes=[
             pltpu.VMEM((2, ny, nz), f32),
-            pltpu.VMEM((2, nx, TILE, nz), f32),
+            pltpu.VMEM((2, nx, nz), f32),
             pltpu.VMEM((2, ny, nz), bf16),
             pltpu.VMEM((2, nx, TILE, nz), bf16),
             pltpu.VMEM((ny, nz), f32),
-            pltpu.VMEM((nx, TILE, nz), f32),
+            pltpu.VMEM((nx, nz), f32),
             pltpu.SemaphoreType.DMA((10,)),
         ],
     )(
@@ -306,23 +345,29 @@
     sends, flat, vert_inverse = lax.optimization_barrier((sends, flat, vert_inverse))
     u, v, w, th, rho, coef = flat
     halo = swapped(sends)
-    h, g, mat = call(
+    h, g, mat, u, v, th, coef = call(
         prepare_kernel,
         "prepare",
         nx * ny,
-        in_specs=[vmem] * 5,
-        out_specs=[vmem] * 3,
-        out_shape=(field, field, jax.ShapeDtypeStruct((3 * order, order), bf16)),
-    )(vert_inverse, u, v, th, coef)
-    for _ in range(SUBSTEPS - 1):
-        sends = call(
-            edges_kernel,
+        in_specs=[hbm] * 5,
+        out_specs=[vmem] * 7,
+        out_shape=(field, field, jax.ShapeDtypeStruct((3 * order, order), bf16))
+        + (field,) * 3
+        + (jax.ShapeDtypeStruct((nx * ny, nz), bf16),),
+        scratch_shapes=[pltpu.VMEM((order, order), f32), pltpu.SemaphoreType.DMA((5,))],
+    )(*(pltpu.with_memory_space_constraint(x, pltpu.HBM) for x in (vert_inverse, u, v, th, coef)))
+    edge_state = tuple(array.reshape(nx, ny, nz) for array in (h, w, th, g))
+    for substep in range(SUBSTEPS - 1):
+        kept = 4 if substep < SUBSTEPS - 2 else 0
+        new_state = call(
+            functools.partial(edges_kernel, substep > 0),
             "edges",
             edge_columns,
-            in_specs=[vmem] * 10,
-            out_specs=[vmem] * 4,
-            out_shape=planes,
-        )(mat, coef_edges, *(array.reshape(nx, ny, nz) for array in (h, g, w, th)), *halo)
+            in_specs=[vmem] * 11,
+            out_specs=[vmem] * (4 + kept),
+            out_shape=planes + (jax.ShapeDtypeStruct((edge_columns, nz), f32),) * kept,
+        )(mat, coef_edges, *edge_state, g.reshape(nx, ny, nz), *halo)
+        sends, edge_state = new_state[:4], new_state[4:]
         arrived = swapped(sends)
         g, h, w, th, u, v, rho = call(
             block_kernel,
@@ -342,7 +387,7 @@
         out_specs=[hbm] * 5,
         out_shape=(field,) * 5,
         scratch_shapes=[pltpu.VMEM((nx * ny, nz), f32)] * 5
-        + [pltpu.SemaphoreType.DMA((4 + 3 * (nx // ROWS),))],
+        + [pltpu.SemaphoreType.DMA((5 * len(last_pieces(nx)),))],
     )(mat, g, h, w, th, u, v, rho, *halo)
     return tuple(out.reshape(nx, ny, nz) for out in outs)
 

time: 52.6 us -> 51.7 us (0.983)
  local copies, waits for them, and re-layouts: 1.25 us -> 0.01 us
  Pallas kernels: 21 us -> 21.9 us
    pallas_call x6, Pallas kernels: 3.76 us -> 5.3 us  [the longest x5 2.83 us: body(): call(functools.partial(edges_kernel, substep > 0), 'edges', edge_columns,...]
    unnamed x14 -> x4, local copies, waits for them, and re-layouts: 1.25 us -> 0.01 us
  transfers between devices with their start and end apart: 24 -> 24, of which waited for: 10 -> 9; matrix products, arithmetic and copies ran while one was open for 0% -> 0% of each run, Pallas kernels for 24% -> 28%
where the time goes in v1:
time: 51.7 us; the launch traced here: 51.5 us
  starting transfers between devices  24.9 us (48%)
  Pallas kernels  21.9 us (42%)
  waiting for transfers between devices  3.67 us (7%)
  between operations  0.98 us (2%)
    ppermute x24, starting transfers between devices, paired(): return lax.ppermute(block, axis, route)  24.9 us
    pallas_call x5, Pallas kernels, body(): call(block_kernel, 'block', nx * ny, in_specs=[vmem] * 13, out_specs=[vme...  11.9 us
    ppermute x24, waiting for transfers between devices, paired(): return lax.ppermute(block, axis, route)  3.67 us
    pallas_call x1, Pallas kernels, body(): call(last_kernel, 'last', nx * ny, limit=24, in_specs=[vmem] * 12, out_sp...  3.45 us
    pallas_call x5, Pallas kernels, body(): call(functools.partial(edges_kernel, substep > 0), 'edges', edge_columns,...  2.83 us
    pallas_call x1, Pallas kernels, body(): call(prepare_kernel, 'prepare', nx * ny, in_specs=[hbm] * 5, out_specs=[v...  2.48 us
    pallas_call x1, Pallas kernels, body(): call(first_edges_kernel, 'first_edges', edge_columns, in_specs=[hbm] * 4,...  1.23 us
  transfers between devices with their start and end apart: 24, of which 9 were waited for; matrix products, arithmetic and copies ran while one was open for 0% of the time, Pallas kernels for 28%

profile of v1, /device:TPU:0, one launch (start us, length us, event | category | flops | bytes accessed | tf_op | source)
XLA Modules:
  0.0 51.5 jit_solution(2723342193068293903)
XLA Ops:
  0.6 1.2 %first_edges.1 = (f32[32,256]{1,0:T(8,128)S(1)}, f32[32,256]{1,0:T(8,128)S(1)}, f32[32,256]{1,0:T(8,128)S(1)}, f32[32,256]{1,0:T(8,128)S(1)}, f32[128,256]{1,0:T(8,128)S(1)}) custom-call(f32[32,32,256]{2,1,0:T(8,128)} %refs_0_.1, bf16[32,32,256]{2,1,0:T(8,128)(2,1)} %refs_1_.1, f32[32,32,256]{2,1,0:T(8,128)} %refs_2_.1, f32[32,32,256]{2,1,0:T(8,128)} %refs_3_.1), custom_call_target="tpu_custom_call" | custom-call | flops 201326592 | bytes 131072 | tf_op jit(solution)/shard_map/first_edges/pallas_call | solution.py:321
  1.9 4.6 %collective-permute-start = (f32[32,256]{1,0:T(8,128)S(1)}, f32[32,256]{1,0:T(8,128)S(1)}, u32[]{:S(2)}, u32[]{:S(2)}) collective-permute-start(f32[32,256]{1,0:T(8,128)S(1)} %get-tuple-element.122), channel_id=1, source_target_pairs={{1,2},{2,1},{3,4},{4,3},{5,6},{6,5},{7,0},{0,7},{9,10},{10,9},{11,... | collective-permute-start | bytes 98312 | tf_op jit(solution)/shard_map/ppermute | solution.py:28
  6.5 2.4 %collective-permute-start.1 = (f32[32,256]{1,0:T(8,128)S(1)}, f32[32,256]{1,0:T(8,128)S(1)}, u32[]{:S(2)}, u32[]{:S(2)}) collective-permute-start(f32[32,256]{1,0:T(8,128)S(1)} %get-tuple-element.123), channel_id=1, source_target_pairs={{8,16},{16,8},{24,0},{0,24},{9,17},{17,9},{25,1},{1,25},{10,18},{1... | collective-permute-start | bytes 98312 | tf_op jit(solution)/shard_map/ppermute | solution.py:28
  9.4 2.5 %prepare.1 = (f32[1024,256]{1,0:T(8,128)S(1)}, f32[1024,256]{1,0:T(8,128)S(1)}, bf16[1536,512]{1,0:T(8,128)(2,1)S(1)}, f32[1024,256]{1,0:T(8,128)S(1)}, f32[1024...) custom-call(f32[512,512]{1,0:T(8,128)} %refs_0_.2, f32[1024,256]{1,0:T(8,128)} %bitcast.29, ...), custom_call_target="tpu_custom_call" | custom-call | flops 1610612736 | bytes 1048576 | tf_op jit(solution)/shard_map/prepare/pallas_call | solution.py:348
  12.0 0.9 %collective-permute-done.2.refs_11_.refs_9_ = f32[32,256]{1,0:T(8,128)S(1)} collective-permute-done((f32[32,256]{1,0:T(8,128)S(1)}, f32[32,256]{1,0:T(8,128)S(1)}, u32[]{:S(2)}, u32[]{:S(2)}) %collective-permute-start.2) | collective-permute-done | bytes 32800 | tf_op jit(solution)/shard_map/ppermute | solution.py:28
  13.5 1.3 %collective-permute-start.5 = (f32[32,256]{1,0:T(8,128)S(1)}, f32[32,256]{1,0:T(8,128)S(1)}, u32[]{:S(2)}, u32[]{:S(2)}) collective-permute-start(f32[32,256]{1,0:T(8,128)S(1)} %get-tuple-element.135), channel_id=1, source_target_pairs={{8,16},{16,8},{24,0},{0,24},{9,17},{17,9},{25,1},{1,25},{10,18},{1... | collective-permute-start | bytes 98312 | tf_op jit(solution)/shard_map/ppermute | solution.py:28
  14.9 0.7 %collective-permute-start.6 = (f32[32,256]{1,0:T(8,128)S(1)}, f32[32,256]{1,0:T(8,128)S(1)}, u32[]{:S(2)}, u32[]{:S(2)}) collective-permute-start(f32[32,256]{1,0:T(8,128)S(1)} %get-tuple-element.136), channel_id=1, source_target_pairs={{0,8},{8,0},{16,24},{24,16},{1,9},{9,1},{17,25},{25,17},{2,10},{10... | collective-permute-start | bytes 98312 | tf_op jit(solution)/shard_map/ppermute | solution.py:28
  15.6 2.4 %block.5 = (f32[1024,256]{1,0:T(8,128)S(1)}, f32[1024,256]{1,0:T(8,128)S(1)}, f32[1024,256]{1,0:T(8,128)S(1)}, f32[1024,256]{1,0:T(8,128)S(1)}, f32[1024,256]{1,...) custom-call(bf16[1536,512]{1,0:T(8,128)(2,1)S(1)} %get-tuple-element.113.refs_0_, ...), custom_call_target="tpu_custom_call" | custom-call | flops 1610612736 | bytes 1048576 | tf_op jit(solution)/shard_map/block/pallas_call | solution.py:372
  19.3 2.2 %collective-permute-start.8 = (f32[32,256]{1,0:T(8,128)S(1)}, f32[32,256]{1,0:T(8,128)S(1)}, u32[]{:S(2)}, u32[]{:S(2)}) collective-permute-start(f32[32,256]{1,0:T(8,128)S(1)} %get-tuple-element.149), channel_id=1, source_target_pairs={{1,2},{2,1},{3,4},{4,3},{5,6},{6,5},{7,0},{0,7},{9,10},{10,9},{11,... | collective-permute-start | bytes 98312 | tf_op jit(solution)/shard_map/ppermute | solution.py:28
  21.5 1.6 %collective-permute-start.9 = (f32[32,256]{1,0:T(8,128)S(1)}, f32[32,256]{1,0:T(8,128)S(1)}, u32[]{:S(2)}, u32[]{:S(2)}) collective-permute-start(f32[32,256]{1,0:T(8,128)S(1)} %get-tuple-element.150), channel_id=1, source_target_pairs={{8,16},{16,8},{24,0},{0,24},{9,17},{17,9},{25,1},{1,25},{10,18},{1... | collective-permute-start | bytes 98312 | tf_op jit(solution)/shard_map/ppermute | solution.py:28
  23.1 1.4 %collective-permute-start.10 = (f32[32,256]{1,0:T(8,128)S(1)}, f32[32,256]{1,0:T(8,128)S(1)}, u32[]{:S(2)}, u32[]{:S(2)}) collective-permute-start(f32[32,256]{1,0:T(8,128)S(1)} %get-tuple-element.151), channel_id=1, source_target_pairs={{0,8},{8,0},{16,24},{24,16},{1,9},{9,1},{17,25},{25,17},{2,10},{10... | collective-permute-start | bytes 98312 | tf_op jit(solution)/shard_map/ppermute | solution.py:28
  24.5 2.4 %block.6 = (f32[1024,256]{1,0:T(8,128)S(1)}, f32[1024,256]{1,0:T(8,128)S(1)}, f32[1024,256]{1,0:T(8,128)S(1)}, f32[1024,256]{1,0:T(8,128)S(1)}, f32[1024,256]{1,...) custom-call(bf16[1536,512]{1,0:T(8,128)(2,1)S(1)} %get-tuple-element.113.refs_0_, ...), custom_call_target="tpu_custom_call" | custom-call | flops 1610612736 | bytes 1048576 | tf_op jit(solution)/shard_map/block/pallas_call | solution.py:372
  27.5 0.8 %collective-permute-start.12 = (f32[32,256]{1,0:T(8,128)S(1)}, f32[32,256]{1,0:T(8,128)S(1)}, u32[]{:S(2)}, u32[]{:S(2)}) collective-permute-start(f32[32,256]{1,0:T(8,128)S(1)} %get-tuple-element.164), channel_id=1, source_target_pairs={{1,2},{2,1},{3,4},{4,3},{5,6},{6,5},{7,0},{0,7},{9,10},{10,9},{11,... | collective-permute-start | bytes 98312 | tf_op jit(solution)/shard_map/ppermute | solution.py:28
  28.4 1.0 %collective-permute-start.13 = (f32[32,256]{1,0:T(8,128)S(1)}, f32[32,256]{1,0:T(8,128)S(1)}, u32[]{:S(2)}, u32[]{:S(2)}) collective-permute-start(f32[32,256]{1,0:T(8,128)S(1)} %get-tuple-element.165), channel_id=1, source_target_pairs={{8,16},{16,8},{24,0},{0,24},{9,17},{17,9},{25,1},{1,25},{10,18},{1... | collective-permute-start | bytes 98312 | tf_op jit(solution)/shard_map/ppermute | solution.py:28
  29.4 1.0 %collective-permute-start.14 = (f32[32,256]{1,0:T(8,128)S(1)}, f32[32,256]{1,0:T(8,128)S(1)}, u32[]{:S(2)}, u32[]{:S(2)}) collective-permute-start(f32[32,256]{1,0:T(8,128)S(1)} %get-tuple-element.166), channel_id=1, source_target_pairs={{0,8},{8,0},{16,24},{24,16},{1,9},{9,1},{17,25},{25,17},{2,10},{10... | collective-permute-start | bytes 98312 | tf_op jit(solution)/shard_map/ppermute | solution.py:28
  30.4 2.4 %block.7 = (f32[1024,256]{1,0:T(8,128)S(1)}, f32[1024,256]{1,0:T(8,128)S(1)}, f32[1024,256]{1,0:T(8,128)S(1)}, f32[1024,256]{1,0:T(8,128)S(1)}, f32[1024,256]{1,...) custom-call(bf16[1536,512]{1,0:T(8,128)(2,1)S(1)} %get-tuple-element.113.refs_0_, ...), custom_call_target="tpu_custom_call" | custom-call | flops 1610612736 | bytes 1048576 | tf_op jit(solution)/shard_map/block/pallas_call | solution.py:372
  33.8 2.1 %collective-permute-start.16 = (f32[32,256]{1,0:T(8,128)S(1)}, f32[32,256]{1,0:T(8,128)S(1)}, u32[]{:S(2)}, u32[]{:S(2)}) collective-permute-start(f32[32,256]{1,0:T(8,128)S(1)} %get-tuple-element.179), channel_id=1, source_target_pairs={{1,2},{2,1},{3,4},{4,3},{5,6},{6,5},{7,0},{0,7},{9,10},{10,9},{11,... | collective-permute-start | bytes 98312 | tf_op jit(solution)/shard_map/ppermute | solution.py:28
  35.9 2.0 %collective-permute-start.17 = (f32[32,256]{1,0:T(8,128)S(1)}, f32[32,256]{1,0:T(8,128)S(1)}, u32[]{:S(2)}, u32[]{:S(2)}) collective-permute-start(f32[32,256]{1,0:T(8,128)S(1)} %get-tuple-element.180), channel_id=1, source_target_pairs={{8,16},{16,8},{24,0},{0,24},{9,17},{17,9},{25,1},{1,25},{10,18},{1... | collective-permute-start | bytes 98312 | tf_op jit(solution)/shard_map/ppermute | solution.py:28
  38.6 2.4 %block.8 = (f32[1024,256]{1,0:T(8,128)S(1)}, f32[1024,256]{1,0:T(8,128)S(1)}, f32[1024,256]{1,0:T(8,128)S(1)}, f32[1024,256]{1,0:T(8,128)S(1)}, f32[1024,256]{1,...) custom-call(bf16[1536,512]{1,0:T(8,128)(2,1)S(1)} %get-tuple-element.113.refs_0_, ...), custom_call_target="tpu_custom_call" | custom-call | flops 1610612736 | bytes 1048576 | tf_op jit(solution)/shard_map/block/pallas_call | solution.py:372
  41.0 0.9 %collective-permute-done.18.refs_11_.refs_9_ = f32[32,256]{1,0:T(8,128)S(1)} collective-permute-done((f32[32,256]{1,0:T(8,128)S(1)}, f32[32,256]{1,0:T(8,128)S(1)}, u32[]{:S(2)}, u32[]{:S(2)}) %collective-permute-start.18) | collective-permute-done | bytes 32800 | tf_op jit(solution)/shard_map/ppermute | solution.py:28
  43.1 0.9 %collective-permute-start.21 = (f32[32,256]{1,0:T(8,128)S(1)}, f32[32,256]{1,0:T(8,128)S(1)}, u32[]{:S(2)}, u32[]{:S(2)}) collective-permute-start(f32[32,256]{1,0:T(8,128)S(1)} %get-tuple-element.195), channel_id=1, source_target_pairs={{8,16},{16,8},{24,0},{0,24},{9,17},{17,9},{25,1},{1,25},{10,18},{1... | collective-permute-start | bytes 98312 | tf_op jit(solution)/shard_map/ppermute | solution.py:28
  44.0 1.1 %collective-permute-start.22 = (f32[32,256]{1,0:T(8,128)S(1)}, f32[32,256]{1,0:T(8,128)S(1)}, u32[]{:S(2)}, u32[]{:S(2)}) collective-permute-start(f32[32,256]{1,0:T(8,128)S(1)} %get-tuple-element.196), channel_id=1, source_target_pairs={{0,8},{8,0},{16,24},{24,16},{1,9},{9,1},{17,25},{25,17},{2,10},{10... | collective-permute-start | bytes 98312 | tf_op jit(solution)/shard_map/ppermute | solution.py:28
  45.0 2.4 %block.9 = (f32[1024,256]{1,0:T(8,128)S(1)}, f32[1024,256]{1,0:T(8,128)S(1)}, f32[1024,256]{1,0:T(8,128)S(1)}, f32[1024,256]{1,0:T(8,128)S(1)}, f32[1024,256]{1,...) custom-call(bf16[1536,512]{1,0:T(8,128)(2,1)S(1)} %get-tuple-element.113.refs_0_, ...), custom_call_target="tpu_custom_call" | custom-call | flops 1610612736 | bytes 1048576 | tf_op jit(solution)/shard_map/block/pallas_call | solution.py:372
  47.9 3.5 %last.1 = (f32[1024,256]{1,0:T(8,128)}, f32[1024,256]{1,0:T(8,128)}, f32[1024,256]{1,0:T(8,128)}, f32[1024,256]{1,0:T(8,128)}, f32[1024,256]{1,0:T(8,128)}) custom-call(bf16[1536,512]{1,0:T(8,128)(2,1)S(1)} %get-tuple-element.113.refs_0_, f32[1024,256]{1,0:T(8,128)S(1)} %get-tuple-element.183.refs_1_, f32[1024,256]{1,0:T(8,128)S(1)} %get-tuple-element.184.refs_2_, ...), custom_call_target="tpu_custom_call" | custom-call | flops 1610612736 | bytes 1048576 | tf_op jit(solution)/shard_map/last/pallas_call | solution.py:381
  (41 shorter events, 6.6 us)
Async XLA Ops:
  1.9 10.1 %collective-permute-start = (f32[32,256]{1,0:T(8,128)S(1)}, f32[32,256]{1,0:T(8,128)S(1)}, u32[]{:S(2)}, u32[]{:S(2)}) collective-permute-start(f32[32,256]{1,0:T(8,128)S(1)} %get-tuple-element.122), channel_id=1, source_target_pairs={{1,2},{2,1},{3,4},{4,3},{5,6},{6,5},{7,0},{0,7},{9,10},{10,9},{11,... | collective-permute-start | bytes 98312 | tf_op jit(solution)/shard_map/ppermute | solution.py:28
  6.5 5.5 %collective-permute-start.1 = (f32[32,256]{1,0:T(8,128)S(1)}, f32[32,256]{1,0:T(8,128)S(1)}, u32[]{:S(2)}, u32[]{:S(2)}) collective-permute-start(f32[32,256]{1,0:T(8,128)S(1)} %get-tuple-element.123), channel_id=1, source_target_pairs={{8,16},{16,8},{24,0},{0,24},{9,17},{17,9},{25,1},{1,25},{10,18},{1... | collective-permute-start | bytes 98312 | tf_op jit(solution)/shard_map/ppermute | solution.py:28
  8.9 3.9 %collective-permute-start.2 = (f32[32,256]{1,0:T(8,128)S(1)}, f32[32,256]{1,0:T(8,128)S(1)}, u32[]{:S(2)}, u32[]{:S(2)}) collective-permute-start(f32[32,256]{1,0:T(8,128)S(1)} %get-tuple-element.124), channel_id=1, source_target_pairs={{0,8},{8,0},{16,24},{24,16},{1,9},{9,1},{17,25},{25,17},{2,10},{10... | collective-permute-start | bytes 98312 | tf_op jit(solution)/shard_map/ppermute | solution.py:28
  9.4 3.4 %collective-permute-start.3 = (f32[32,256]{1,0:T(8,128)S(1)}, f32[32,256]{1,0:T(8,128)S(1)}, u32[]{:S(2)}, u32[]{:S(2)}) collective-permute-start(f32[32,256]{1,0:T(8,128)S(1)} %get-tuple-element.125), channel_id=1, source_target_pairs={{0,1},{1,0},{2,3},{3,2},{4,5},{5,4},{6,7},{7,6},{8,9},{9,8},{10,11... | collective-permute-start | bytes 98312 | tf_op jit(solution)/shard_map/ppermute | solution.py:28
  13.5 5.2 %collective-permute-start.4 = (f32[32,256]{1,0:T(8,128)S(1)}, f32[32,256]{1,0:T(8,128)S(1)}, u32[]{:S(2)}, u32[]{:S(2)}) collective-permute-start(f32[32,256]{1,0:T(8,128)S(1)} %get-tuple-element.134), channel_id=1, source_target_pairs={{1,2},{2,1},{3,4},{4,3},{5,6},{6,5},{7,0},{0,7},{9,10},{10,9},{11,... | collective-permute-start | bytes 98312 | tf_op jit(solution)/shard_map/ppermute | solution.py:28
  13.5 5.1 %collective-permute-start.5 = (f32[32,256]{1,0:T(8,128)S(1)}, f32[32,256]{1,0:T(8,128)S(1)}, u32[]{:S(2)}, u32[]{:S(2)}) collective-permute-start(f32[32,256]{1,0:T(8,128)S(1)} %get-tuple-element.135), channel_id=1, source_target_pairs={{8,16},{16,8},{24,0},{0,24},{9,17},{17,9},{25,1},{1,25},{10,18},{1... | collective-permute-start | bytes 98312 | tf_op jit(solution)/shard_map/ppermute | solution.py:28
  14.9 3.9 %collective-permute-start.6 = (f32[32,256]{1,0:T(8,128)S(1)}, f32[32,256]{1,0:T(8,128)S(1)}, u32[]{:S(2)}, u32[]{:S(2)}) collective-permute-start(f32[32,256]{1,0:T(8,128)S(1)} %get-tuple-element.136), channel_id=1, source_target_pairs={{0,8},{8,0},{16,24},{24,16},{1,9},{9,1},{17,25},{25,17},{2,10},{10... | collective-permute-start | bytes 98312 | tf_op jit(solution)/shard_map/ppermute | solution.py:28
  15.6 3.2 %collective-permute-start.7 = (f32[32,256]{1,0:T(8,128)S(1)}, f32[32,256]{1,0:T(8,128)S(1)}, u32[]{:S(2)}, u32[]{:S(2)}) collective-permute-start(f32[32,256]{1,0:T(8,128)S(1)} %get-tuple-element.137), channel_id=1, source_target_pairs={{0,1},{1,0},{2,3},{3,2},{4,5},{5,4},{6,7},{7,6},{8,9},{9,8},{10,11... | collective-permute-start | bytes 98312 | tf_op jit(solution)/shard_map/ppermute | solution.py:28
  19.3 7.6 %collective-permute-start.8 = (f32[32,256]{1,0:T(8,128)S(1)}, f32[32,256]{1,0:T(8,128)S(1)}, u32[]{:S(2)}, u32[]{:S(2)}) collective-permute-start(f32[32,256]{1,0:T(8,128)S(1)} %get-tuple-element.149), channel_id=1, source_target_pairs={{1,2},{2,1},{3,4},{4,3},{5,6},{6,5},{7,0},{0,7},{9,10},{10,9},{11,... | collective-permute-start | bytes 98312 | tf_op jit(solution)/shard_map/ppermute | solution.py:28
  21.5 5.4 %collective-permute-start.9 = (f32[32,256]{1,0:T(8,128)S(1)}, f32[32,256]{1,0:T(8,128)S(1)}, u32[]{:S(2)}, u32[]{:S(2)}) collective-permute-start(f32[32,256]{1,0:T(8,128)S(1)} %get-tuple-element.150), channel_id=1, source_target_pairs={{8,16},{16,8},{24,0},{0,24},{9,17},{17,9},{25,1},{1,25},{10,18},{1... | collective-permute-start | bytes 98312 | tf_op jit(solution)/shard_map/ppermute | solution.py:28
  23.1 3.9 %collective-permute-start.10 = (f32[32,256]{1,0:T(8,128)S(1)}, f32[32,256]{1,0:T(8,128)S(1)}, u32[]{:S(2)}, u32[]{:S(2)}) collective-permute-start(f32[32,256]{1,0:T(8,128)S(1)} %get-tuple-element.151), channel_id=1, source_target_pairs={{0,8},{8,0},{16,24},{24,16},{1,9},{9,1},{17,25},{25,17},{2,10},{10... | collective-permute-start | bytes 98312 | tf_op jit(solution)/shard_map/ppermute | solution.py:28
  24.5 2.5 %collective-permute-start.11 = (f32[32,256]{1,0:T(8,128)S(1)}, f32[32,256]{1,0:T(8,128)S(1)}, u32[]{:S(2)}, u32[]{:S(2)}) collective-permute-start(f32[32,256]{1,0:T(8,128)S(1)} %get-tuple-element.152), channel_id=1, source_target_pairs={{0,1},{1,0},{2,3},{3,2},{4,5},{5,4},{6,7},{7,6},{8,9},{9,8},{10,11... | collective-permute-start | bytes 98312 | tf_op jit(solution)/shard_map/ppermute | solution.py:28
  27.5 5.2 %collective-permute-start.12 = (f32[32,256]{1,0:T(8,128)S(1)}, f32[32,256]{1,0:T(8,128)S(1)}, u32[]{:S(2)}, u32[]{:S(2)}) collective-permute-start(f32[32,256]{1,0:T(8,128)S(1)} %get-tuple-element.164), channel_id=1, source_target_pairs={{1,2},{2,1},{3,4},{4,3},{5,6},{6,5},{7,0},{0,7},{9,10},{10,9},{11,... | collective-permute-start | bytes 98312 | tf_op jit(solution)/shard_map/ppermute | solution.py:28
  28.4 4.8 %collective-permute-start.13 = (f32[32,256]{1,0:T(8,128)S(1)}, f32[32,256]{1,0:T(8,128)S(1)}, u32[]{:S(2)}, u32[]{:S(2)}) collective-permute-start(f32[32,256]{1,0:T(8,128)S(1)} %get-tuple-element.165), channel_id=1, source_target_pairs={{8,16},{16,8},{24,0},{0,24},{9,17},{17,9},{25,1},{1,25},{10,18},{1... | collective-permute-start | bytes 98312 | tf_op jit(solution)/shard_map/ppermute | solution.py:28
  29.4 3.9 %collective-permute-start.14 = (f32[32,256]{1,0:T(8,128)S(1)}, f32[32,256]{1,0:T(8,128)S(1)}, u32[]{:S(2)}, u32[]{:S(2)}) collective-permute-start(f32[32,256]{1,0:T(8,128)S(1)} %get-tuple-element.166), channel_id=1, source_target_pairs={{0,8},{8,0},{16,24},{24,16},{1,9},{9,1},{17,25},{25,17},{2,10},{10... | collective-permute-start | bytes 98312 | tf_op jit(solution)/shard_map/ppermute | solution.py:28
  30.4 2.9 %collective-permute-start.15 = (f32[32,256]{1,0:T(8,128)S(1)}, f32[32,256]{1,0:T(8,128)S(1)}, u32[]{:S(2)}, u32[]{:S(2)}) collective-permute-start(f32[32,256]{1,0:T(8,128)S(1)} %get-tuple-element.167), channel_id=1, source_target_pairs={{0,1},{1,0},{2,3},{3,2},{4,5},{5,4},{6,7},{7,6},{8,9},{9,8},{10,11... | collective-permute-start | bytes 98312 | tf_op jit(solution)/shard_map/ppermute | solution.py:28
  33.8 7.2 %collective-permute-start.16 = (f32[32,256]{1,0:T(8,128)S(1)}, f32[32,256]{1,0:T(8,128)S(1)}, u32[]{:S(2)}, u32[]{:S(2)}) collective-permute-start(f32[32,256]{1,0:T(8,128)S(1)} %get-tuple-element.179), channel_id=1, source_target_pairs={{1,2},{2,1},{3,4},{4,3},{5,6},{6,5},{7,0},{0,7},{9,10},{10,9},{11,... | collective-permute-start | bytes 98312 | tf_op jit(solution)/shard_map/ppermute | solution.py:28
  35.9 5.1 %collective-permute-start.17 = (f32[32,256]{1,0:T(8,128)S(1)}, f32[32,256]{1,0:T(8,128)S(1)}, u32[]{:S(2)}, u32[]{:S(2)}) collective-permute-start(f32[32,256]{1,0:T(8,128)S(1)} %get-tuple-element.180), channel_id=1, source_target_pairs={{8,16},{16,8},{24,0},{0,24},{9,17},{17,9},{25,1},{1,25},{10,18},{1... | collective-permute-start | bytes 98312 | tf_op jit(solution)/shard_map/ppermute | solution.py:28
  37.9 3.9 %collective-permute-start.18 = (f32[32,256]{1,0:T(8,128)S(1)}, f32[32,256]{1,0:T(8,128)S(1)}, u32[]{:S(2)}, u32[]{:S(2)}) collective-permute-start(f32[32,256]{1,0:T(8,128)S(1)} %get-tuple-element.181), channel_id=1, source_target_pairs={{0,8},{8,0},{16,24},{24,16},{1,9},{9,1},{17,25},{25,17},{2,10},{10... | collective-permute-start | bytes 98312 | tf_op jit(solution)/shard_map/ppermute | solution.py:28
  38.6 3.3 %collective-permute-start.19 = (f32[32,256]{1,0:T(8,128)S(1)}, f32[32,256]{1,0:T(8,128)S(1)}, u32[]{:S(2)}, u32[]{:S(2)}) collective-permute-start(f32[32,256]{1,0:T(8,128)S(1)} %get-tuple-element.182), channel_id=1, source_target_pairs={{0,1},{1,0},{2,3},{3,2},{4,5},{5,4},{6,7},{7,6},{8,9},{9,8},{10,11... | collective-permute-start | bytes 98312 | tf_op jit(solution)/shard_map/ppermute | solution.py:28
  42.5 5.2 %collective-permute-start.20 = (f32[32,256]{1,0:T(8,128)S(1)}, f32[32,256]{1,0:T(8,128)S(1)}, u32[]{:S(2)}, u32[]{:S(2)}) collective-permute-start(f32[32,256]{1,0:T(8,128)S(1)} %get-tuple-element.194), channel_id=1, source_target_pairs={{1,2},{2,1},{3,4},{4,3},{5,6},{6,5},{7,0},{0,7},{9,10},{10,9},{11,... | collective-permute-start | bytes 98312 | tf_op jit(solution)/shard_map/ppermute | solution.py:28
  43.1 4.8 %collective-permute-start.21 = (f32[32,256]{1,0:T(8,128)S(1)}, f32[32,256]{1,0:T(8,128)S(1)}, u32[]{:S(2)}, u32[]{:S(2)}) collective-permute-start(f32[32,256]{1,0:T(8,128)S(1)} %get-tuple-element.195), channel_id=1, source_target_pairs={{8,16},{16,8},{24,0},{0,24},{9,17},{17,9},{25,1},{1,25},{10,18},{1... | collective-permute-start | bytes 98312 | tf_op jit(solution)/shard_map/ppermute | solution.py:28
  44.0 3.9 %collective-permute-start.22 = (f32[32,256]{1,0:T(8,128)S(1)}, f32[32,256]{1,0:T(8,128)S(1)}, u32[]{:S(2)}, u32[]{:S(2)}) collective-permute-start(f32[32,256]{1,0:T(8,128)S(1)} %get-tuple-element.196), channel_id=1, source_target_pairs={{0,8},{8,0},{16,24},{24,16},{1,9},{9,1},{17,25},{25,17},{2,10},{10... | collective-permute-start | bytes 98312 | tf_op jit(solution)/shard_map/ppermute | solution.py:28
  45.0 2.9 %collective-permute-start.23 = (f32[32,256]{1,0:T(8,128)S(1)}, f32[32,256]{1,0:T(8,128)S(1)}, u32[]{:S(2)}, u32[]{:S(2)}) collective-permute-start(f32[32,256]{1,0:T(8,128)S(1)} %get-tuple-element.197), channel_id=1, source_target_pairs={{0,1},{1,0},{2,3},{3,2},{4,5},{5,4},{6,7},{7,6},{8,9},{9,8},{10,11... | collective-permute-start | bytes 98312 | tf_op jit(solution)/shard_map/ppermute | solution.py:28
  (2 other events, 13.7 us)

commit v2 on v1

--- a/solution.py
+++ b/solution.py
@@ -14,6 +14,8 @@
 
 MIB = 1024 * 1024
 ROWS = 8
+LAST_ROWS = 4
+FLUX_ROWS = 8
 TILE = 8
 
 ROUTES = (("gy", 1), ("gx", 1), ("gx", 0), ("gy", 0))
@@ -203,14 +205,14 @@
     return mid, west, east, before(mid, south_of(halo, one)), after(mid, north_of(halo, one))
 
 
-def solve_planes(base, count, nx, ny, mat_ref, g_ref, h_ref, w_ref, th_ref, halo):
+def solve_planes(base, count, nx, ny, mat_ref, g_ref, h_ref, w_ref, th_ref, halo, h_out):
     nz = h_ref.shape[1]
-    ws, ths, divs = [], [], []
+    ws, ths = [], []
     for i in range(base, base + count):
         here = pl.ds(i * ny, ny)
         mid, west, east, south, north = around(i, nx, ny, g_ref, halo)
         h = h_ref[here, :] + (west + east) + (south + north) - 4.0 * mid
-        divs.append(h)
+        h_out[here, :] = h
         ws.append(w_ref[here, :])
         ths.append(th_ref[here, :] - courant * h)
     solved = product(jnp.concatenate(ws, axis=0), jnp.concatenate(ths, axis=0), mat_ref)
@@ -218,40 +220,54 @@
         q = solved[k * ny : (k + 1) * ny]
         w, th = q[:, :nz], q[:, nz:]
         here = pl.ds((base + k) * ny, ny)
-        yield here, divs[k], w, th, divs[k] + level_difference(w)
+        yield here, w, th, h_out[here, :] + level_difference(w)
 
 
 def block_kernel(
     nx, ny, mat_ref, coef_ref, g_ref, h_ref, w_ref, th_ref, u_ref, v_ref, rho_ref, *refs
 ):
-    halo = refs[:4]
-    g_out, h_out, w_out, th_out, u_out, v_out, rho_out = refs[4:]
-    for base in range(0, nx, ROWS):
-        for i in range(base, base + ROWS):
+    edge_h, edge_w, edge_th, edge_g = refs[:4]
+    halo = refs[4:8]
+    g_out, h_out, w_out, th_out, u_out, v_out, rho_out = refs[8:]
+
+    def fluxes(planes):
+        for i in planes:
             here = pl.ds(i * ny, ny)
             mid, west, _, south, _ = around(i, nx, ny, g_ref, halo)
             u_out[here, :] = u_ref[here, :] + (mid - west)
             v_out[here, :] = v_ref[here, :] + (mid - south)
-        for here, h, w, th, div in solve_planes(
-            base, ROWS, nx, ny, mat_ref, g_ref, h_ref, w_ref, th_ref, halo
+
+    for side, i in enumerate((0, nx - 1)):
+        here, there = pl.ds(i * ny, ny), pl.ds(side * ny, ny)
+        h, w = edge_h[there, :], edge_w[there, :]
+        h_out[here, :] = h
+        w_out[here, :] = w
+        th_out[here, :] = edge_th[there, :]
+        g_out[here, :] = edge_g[there, :]
+        rho_out[here, :] = rho_ref[here, :] - courant * (h + level_difference(w))
+    fluxes((0, nx - 1))
+    for base in range(1, nx - 1, ROWS):
+        count = min(ROWS, nx - 1 - base)
+        fluxes(range(base, base + count))
+        for here, w, th, div in solve_planes(
+            base, count, nx, ny, mat_ref, g_ref, h_ref, w_ref, th_ref, halo, h_out
         ):
-            h_out[here, :] = h
             rho_out[here, :] = rho_ref[here, :] - courant * div
             w_out[here, :] = w
             th_out[here, :] = th
             g_out[here, :] = damping * div - courant * (coef_ref[here, :].astype(jnp.float32) * th)
 
 
-def last_pieces(nx):
-    pieces = [(base, ROWS) for base in range(0, nx - ROWS, ROWS)]
-    half = ROWS // 2
-    return pieces + [(nx - ROWS, half), (nx - half, half)]
-
-
 def last_kernel(nx, ny, mat_ref, g_ref, h_ref, w_ref, th_ref, u_ref, v_ref, rho_ref, *refs):
-    halo, outs, parts, sems = refs[:4], refs[4:9], refs[9:14], refs[14]
+    halo, outs, parts = refs[:4], refs[4:9], refs[9:14]
+    sems, flux_sems = refs[14:]
     rho_part, u_part, v_part, w_part, th_part = parts
     copies = []
+
+    def flux_copy(slot, rows, sem):
+        return pltpu.make_async_copy(
+            parts[slot].at[rows, :], outs[slot].at[rows, :], flux_sems.at[sem]
+        )
 
     def send(slot, start, count):
         rows = pl.ds(start * ny, count * ny)
@@ -262,30 +278,37 @@
         )
         copies[-1].start()
 
-    def fluxes(base, count):
-        for i in range(base, base + count):
-            here = pl.ds(i * ny, ny)
-            mid, west, _, south, _ = around(i, nx, ny, g_ref, halo)
+    @pl.loop(0, nx // FLUX_ROWS)
+    def fluxes(step):
+        base = step * FLUX_ROWS
+        for k in range(FLUX_ROWS):
+            i = base + k
+            here = pl.ds(pl.multiple_of(i * ny, ny), ny)
+            mid = g_ref[here, :]
+            back = jnp.maximum(i - 1, 0) if k == 0 else i - 1
+            west = g_ref[pl.ds(pl.multiple_of(back * ny, ny), ny), :]
+            if k == 0:
+                west = jnp.where(base == 0, west_of(halo), west)
+            south = before(mid, south_of(halo, pl.ds(i, 1)))
             u_part[here, :] = u_ref[here, :] + (mid - west)
             v_part[here, :] = v_ref[here, :] + (mid - south)
+        rows = pl.ds(pl.multiple_of(base * ny, FLUX_ROWS * ny), FLUX_ROWS * ny)
         for slot in (1, 2):
-            send(slot, base, count)
-
-    pieces = last_pieces(nx)
-    for base, count in pieces:
-        if base == 0:
-            fluxes(base, count)
-        if base + count < nx:
-            ahead = dict(pieces)[base + count]
-            fluxes(base + count, ahead)
-        for here, _, w, th, div in solve_planes(
-            base, count, nx, ny, mat_ref, g_ref, h_ref, w_ref, th_ref, halo
+            flux_copy(slot, rows, 2 * step + slot - 1).start()
+
+    for base in range(0, nx, LAST_ROWS):
+        for here, w, th, div in solve_planes(
+            base, LAST_ROWS, nx, ny, mat_ref, g_ref, h_ref, w_ref, th_ref, halo, rho_part
         ):
             w_part[here, :] = w
             th_part[here, :] = th
             rho_part[here, :] = rho_ref[here, :] - courant * div
         for slot in (3, 4, 0):
-            send(slot, base, count)
+            send(slot, base, LAST_ROWS)
+    for step in range(nx // FLUX_ROWS):
+        rows = pl.ds(step * FLUX_ROWS * ny, FLUX_ROWS * ny)
+        for slot in (1, 2):
+            flux_copy(slot, rows, 2 * step + slot - 1).wait()
     for copy in copies:
         copy.wait()
 
@@ -358,14 +381,13 @@
     )(*(pltpu.with_memory_space_constraint(x, pltpu.HBM) for x in (vert_inverse, u, v, th, coef)))
     edge_state = tuple(array.reshape(nx, ny, nz) for array in (h, w, th, g))
     for substep in range(SUBSTEPS - 1):
-        kept = 4 if substep < SUBSTEPS - 2 else 0
         new_state = call(
             functools.partial(edges_kernel, substep > 0),
             "edges",
             edge_columns,
             in_specs=[vmem] * 11,
-            out_specs=[vmem] * (4 + kept),
-            out_shape=planes + (jax.ShapeDtypeStruct((edge_columns, nz), f32),) * kept,
+            out_specs=[vmem] * 8,
+            out_shape=planes + (jax.ShapeDtypeStruct((edge_columns, nz), f32),) * 4,
         )(mat, coef_edges, *edge_state, g.reshape(nx, ny, nz), *halo)
         sends, edge_state = new_state[:4], new_state[4:]
         arrived = swapped(sends)
@@ -373,10 +395,10 @@
             block_kernel,
             "block",
             nx * ny,
-            in_specs=[vmem] * 13,
+            in_specs=[vmem] * 17,
             out_specs=[vmem] * 7,
             out_shape=(field,) * 7,
-        )(mat, coef, g, h, w, th, u, v, rho, *halo)
+        )(mat, coef, g, h, w, th, u, v, rho, *edge_state, *halo)
         halo = arrived
     outs = call(
         last_kernel,
@@ -387,7 +409,10 @@
         out_specs=[hbm] * 5,
         out_shape=(field,) * 5,
         scratch_shapes=[pltpu.VMEM((nx * ny, nz), f32)] * 5
-        + [pltpu.SemaphoreType.DMA((5 * len(last_pieces(nx)),))],
+        + [
+            pltpu.SemaphoreType.DMA((3 * (nx // LAST_ROWS),)),
+            pltpu.SemaphoreType.DMA((2 * (nx // FLUX_ROWS),)),
+        ],
     )(mat, g, h, w, th, u, v, rho, *halo)
     return tuple(out.reshape(nx, ny, nz) for out in outs)
 

time: 51.7 us -> 51.1 us (0.988)
  Pallas kernels: 21.9 us -> 21.1 us
  transfers between devices with their start and end apart: 24 -> 24, of which waited for: 9 -> 11; matrix products, arithmetic and copies ran while one was open for 0% -> 0% of each run, Pallas kernels for 28% -> 27%
where the time goes in v2:
time: 51.1 us; the launch traced here: 50.9 us
  starting transfers between devices  24.8 us (49%)
  Pallas kernels  21.1 us (41%)
  waiting for transfers between devices  4.1 us (8%)
  between operations  0.97 us (2%)
    ppermute x24, starting transfers between devices, paired(): return lax.ppermute(block, axis, route)  24.8 us
    pallas_call x5, Pallas kernels, body(): call(block_kernel, 'block', nx * ny, in_specs=[vmem] * 17, out_specs=[vme...  11.5 us
    ppermute x24, waiting for transfers between devices, paired(): return lax.ppermute(block, axis, route)  4.1 us
    pallas_call x1, Pallas kernels, body(): call(last_kernel, 'last', nx * ny, limit=24, in_specs=[vmem] * 12, out_sp...  3.25 us
    pallas_call x5, Pallas kernels, body(): call(functools.partial(edges_kernel, substep > 0), 'edges', edge_columns,...  2.63 us
    pallas_call x1, Pallas kernels, body(): call(prepare_kernel, 'prepare', nx * ny, in_specs=[hbm] * 5, out_specs=[v...  2.48 us
    pallas_call x1, Pallas kernels, body(): call(first_edges_kernel, 'first_edges', edge_columns, in_specs=[hbm] * 4,...  1.23 us
  transfers between devices with their start and end apart: 24, of which 11 were waited for; matrix products, arithmetic and copies ran while one was open for 0% of the time, Pallas kernels for 27%

profile of v2, /device:TPU:0, one launch (start us, length us, event | category | flops | bytes accessed | tf_op | source)
XLA Modules:
  0.0 50.9 jit_solution(16611287848157833442)
XLA Ops:
  0.6 1.2 %first_edges.1 = (f32[32,256]{1,0:T(8,128)S(1)}, f32[32,256]{1,0:T(8,128)S(1)}, f32[32,256]{1,0:T(8,128)S(1)}, f32[32,256]{1,0:T(8,128)S(1)}, f32[128,256]{1,0:T(8,128)S(1)}) custom-call(f32[32,32,256]{2,1,0:T(8,128)} %refs_0_.1, bf16[32,32,256]{2,1,0:T(8,128)(2,1)} %refs_1_.1, f32[32,32,256]{2,1,0:T(8,128)} %refs_2_.1, f32[32,32,256]{2,1,0:T(8,128)} %refs_3_.1), custom_call_target="tpu_custom_call" | custom-call | flops 201326592 | bytes 131072 | tf_op jit(solution)/shard_map/first_edges/pallas_call | solution.py:344
  1.9 4.6 %collective-permute-start = (f32[32,256]{1,0:T(8,128)S(1)}, f32[32,256]{1,0:T(8,128)S(1)}, u32[]{:S(2)}, u32[]{:S(2)}) collective-permute-start(f32[32,256]{1,0:T(8,128)S(1)} %get-tuple-element.127), channel_id=1, source_target_pairs={{1,2},{2,1},{3,4},{4,3},{5,6},{6,5},{7,0},{0,7},{9,10},{10,9},{11,... | collective-permute-start | bytes 98312 | tf_op jit(solution)/shard_map/ppermute | solution.py:30
  6.5 2.4 %collective-permute-start.1 = (f32[32,256]{1,0:T(8,128)S(1)}, f32[32,256]{1,0:T(8,128)S(1)}, u32[]{:S(2)}, u32[]{:S(2)}) collective-permute-start(f32[32,256]{1,0:T(8,128)S(1)} %get-tuple-element.128), channel_id=1, source_target_pairs={{8,16},{16,8},{24,0},{0,24},{9,17},{17,9},{25,1},{1,25},{10,18},{1... | collective-permute-start | bytes 98312 | tf_op jit(solution)/shard_map/ppermute | solution.py:30
  9.4 2.5 %prepare.1 = (f32[1024,256]{1,0:T(8,128)S(1)}, f32[1024,256]{1,0:T(8,128)S(1)}, bf16[1536,512]{1,0:T(8,128)(2,1)S(1)}, f32[1024,256]{1,0:T(8,128)S(1)}, f32[1024...) custom-call(f32[512,512]{1,0:T(8,128)} %refs_0_.2, f32[1024,256]{1,0:T(8,128)} %bitcast.29, ...), custom_call_target="tpu_custom_call" | custom-call | flops 1610612736 | bytes 1048576 | tf_op jit(solution)/shard_map/prepare/pallas_call | solution.py:371
  12.0 0.9 %collective-permute-done.2.refs_9_.refs_15_ = f32[32,256]{1,0:T(8,128)S(1)} collective-permute-done((f32[32,256]{1,0:T(8,128)S(1)}, f32[32,256]{1,0:T(8,128)S(1)}, u32[]{:S(2)}, u32[]{:S(2)}) %collective-permute-start.2) | collective-permute-done | bytes 32800 | tf_op jit(solution)/shard_map/ppermute | solution.py:30
  13.5 1.3 %collective-permute-start.5 = (f32[32,256]{1,0:T(8,128)S(1)}, f32[32,256]{1,0:T(8,128)S(1)}, u32[]{:S(2)}, u32[]{:S(2)}) collective-permute-start(f32[32,256]{1,0:T(8,128)S(1)} %get-tuple-element.143), channel_id=1, source_target_pairs={{8,16},{16,8},{24,0},{0,24},{9,17},{17,9},{25,1},{1,25},{10,18},{1... | collective-permute-start | bytes 98312 | tf_op jit(solution)/shard_map/ppermute | solution.py:30
  15.6 2.3 %block.5 = (f32[1024,256]{1,0:T(8,128)S(1)}, f32[1024,256]{1,0:T(8,128)S(1)}, f32[1024,256]{1,0:T(8,128)S(1)}, f32[1024,256]{1,0:T(8,128)S(1)}, f32[1024,256]{1,...) custom-call(bf16[1536,512]{1,0:T(8,128)(2,1)S(1)} %get-tuple-element.117.refs_0_, ...), custom_call_target="tpu_custom_call" | custom-call | flops 1610612736 | bytes 1048576 | tf_op jit(solution)/shard_map/block/pallas_call | solution.py:394
  17.9 0.8 %collective-permute-done.4.refs_7_.refs_13_ = f32[32,256]{1,0:T(8,128)S(1)} collective-permute-done((f32[32,256]{1,0:T(8,128)S(1)}, f32[32,256]{1,0:T(8,128)S(1)}, u32[]{:S(2)}, u32[]{:S(2)}) %collective-permute-start.4) | collective-permute-done | bytes 32800 | tf_op jit(solution)/shard_map/ppermute | solution.py:30
  19.3 2.1 %collective-permute-start.8 = (f32[32,256]{1,0:T(8,128)S(1)}, f32[32,256]{1,0:T(8,128)S(1)}, u32[]{:S(2)}, u32[]{:S(2)}) collective-permute-start(f32[32,256]{1,0:T(8,128)S(1)} %get-tuple-element.157), channel_id=1, source_target_pairs={{1,2},{2,1},{3,4},{4,3},{5,6},{6,5},{7,0},{0,7},{9,10},{10,9},{11,... | collective-permute-start | bytes 98312 | tf_op jit(solution)/shard_map/ppermute | solution.py:30
  21.4 1.6 %collective-permute-start.9 = (f32[32,256]{1,0:T(8,128)S(1)}, f32[32,256]{1,0:T(8,128)S(1)}, u32[]{:S(2)}, u32[]{:S(2)}) collective-permute-start(f32[32,256]{1,0:T(8,128)S(1)} %get-tuple-element.158), channel_id=1, source_target_pairs={{8,16},{16,8},{24,0},{0,24},{9,17},{17,9},{25,1},{1,25},{10,18},{1... | collective-permute-start | bytes 98312 | tf_op jit(solution)/shard_map/ppermute | solution.py:30
  23.1 1.4 %collective-permute-start.10 = (f32[32,256]{1,0:T(8,128)S(1)}, f32[32,256]{1,0:T(8,128)S(1)}, u32[]{:S(2)}, u32[]{:S(2)}) collective-permute-start(f32[32,256]{1,0:T(8,128)S(1)} %get-tuple-element.159), channel_id=1, source_target_pairs={{0,8},{8,0},{16,24},{24,16},{1,9},{9,1},{17,25},{25,17},{2,10},{10... | collective-permute-start | bytes 98312 | tf_op jit(solution)/shard_map/ppermute | solution.py:30
  24.4 2.3 %block.6 = (f32[1024,256]{1,0:T(8,128)S(1)}, f32[1024,256]{1,0:T(8,128)S(1)}, f32[1024,256]{1,0:T(8,128)S(1)}, f32[1024,256]{1,0:T(8,128)S(1)}, f32[1024,256]{1,...) custom-call(bf16[1536,512]{1,0:T(8,128)(2,1)S(1)} %get-tuple-element.117.refs_0_, ...), custom_call_target="tpu_custom_call" | custom-call | flops 1610612736 | bytes 1048576 | tf_op jit(solution)/shard_map/block/pallas_call | solution.py:394
  27.5 0.8 %collective-permute-start.12 = (f32[32,256]{1,0:T(8,128)S(1)}, f32[32,256]{1,0:T(8,128)S(1)}, u32[]{:S(2)}, u32[]{:S(2)}) collective-permute-start(f32[32,256]{1,0:T(8,128)S(1)} %get-tuple-element.172), channel_id=1, source_target_pairs={{1,2},{2,1},{3,4},{4,3},{5,6},{6,5},{7,0},{0,7},{9,10},{10,9},{11,... | collective-permute-start | bytes 98312 | tf_op jit(solution)/shard_map/ppermute | solution.py:30
  28.3 1.0 %collective-permute-start.13 = (f32[32,256]{1,0:T(8,128)S(1)}, f32[32,256]{1,0:T(8,128)S(1)}, u32[]{:S(2)}, u32[]{:S(2)}) collective-permute-start(f32[32,256]{1,0:T(8,128)S(1)} %get-tuple-element.173), channel_id=1, source_target_pairs={{8,16},{16,8},{24,0},{0,24},{9,17},{17,9},{25,1},{1,25},{10,18},{1... | collective-permute-start | bytes 98312 | tf_op jit(solution)/shard_map/ppermute | solution.py:30
  29.2 1.0 %collective-permute-start.14 = (f32[32,256]{1,0:T(8,128)S(1)}, f32[32,256]{1,0:T(8,128)S(1)}, u32[]{:S(2)}, u32[]{:S(2)}) collective-permute-start(f32[32,256]{1,0:T(8,128)S(1)} %get-tuple-element.174), channel_id=1, source_target_pairs={{0,8},{8,0},{16,24},{24,16},{1,9},{9,1},{17,25},{25,17},{2,10},{10... | collective-permute-start | bytes 98312 | tf_op jit(solution)/shard_map/ppermute | solution.py:30
  30.3 2.3 %block.7 = (f32[1024,256]{1,0:T(8,128)S(1)}, f32[1024,256]{1,0:T(8,128)S(1)}, f32[1024,256]{1,0:T(8,128)S(1)}, f32[1024,256]{1,0:T(8,128)S(1)}, f32[1024,256]{1,...) custom-call(bf16[1536,512]{1,0:T(8,128)(2,1)S(1)} %get-tuple-element.117.refs_0_, ...), custom_call_target="tpu_custom_call" | custom-call | flops 1610612736 | bytes 1048576 | tf_op jit(solution)/shard_map/block/pallas_call | solution.py:394
  33.7 2.1 %collective-permute-start.16 = (f32[32,256]{1,0:T(8,128)S(1)}, f32[32,256]{1,0:T(8,128)S(1)}, u32[]{:S(2)}, u32[]{:S(2)}) collective-permute-start(f32[32,256]{1,0:T(8,128)S(1)} %get-tuple-element.187), channel_id=1, source_target_pairs={{1,2},{2,1},{3,4},{4,3},{5,6},{6,5},{7,0},{0,7},{9,10},{10,9},{11,... | collective-permute-start | bytes 98312 | tf_op jit(solution)/shard_map/ppermute | solution.py:30
  35.7 2.0 %collective-permute-start.17 = (f32[32,256]{1,0:T(8,128)S(1)}, f32[32,256]{1,0:T(8,128)S(1)}, u32[]{:S(2)}, u32[]{:S(2)}) collective-permute-start(f32[32,256]{1,0:T(8,128)S(1)} %get-tuple-element.188), channel_id=1, source_target_pairs={{8,16},{16,8},{24,0},{0,24},{9,17},{17,9},{25,1},{1,25},{10,18},{1... | collective-permute-start | bytes 98312 | tf_op jit(solution)/shard_map/ppermute | solution.py:30
  38.4 2.3 %block.8 = (f32[1024,256]{1,0:T(8,128)S(1)}, f32[1024,256]{1,0:T(8,128)S(1)}, f32[1024,256]{1,0:T(8,128)S(1)}, f32[1024,256]{1,0:T(8,128)S(1)}, f32[1024,256]{1,...) custom-call(bf16[1536,512]{1,0:T(8,128)(2,1)S(1)} %get-tuple-element.117.refs_0_, ...), custom_call_target="tpu_custom_call" | custom-call | flops 1610612736 | bytes 1048576 | tf_op jit(solution)/shard_map/block/pallas_call | solution.py:394
  40.8 0.9 %collective-permute-done.18.refs_9_.refs_15_ = f32[32,256]{1,0:T(8,128)S(1)} collective-permute-done((f32[32,256]{1,0:T(8,128)S(1)}, f32[32,256]{1,0:T(8,128)S(1)}, u32[]{:S(2)}, u32[]{:S(2)}) %collective-permute-start.18) | collective-permute-done | bytes 32800 | tf_op jit(solution)/shard_map/ppermute | solution.py:30
  42.6 1.0 %collective-permute-start.21 = (f32[32,256]{1,0:T(8,128)S(1)}, f32[32,256]{1,0:T(8,128)S(1)}, u32[]{:S(2)}, u32[]{:S(2)}) collective-permute-start(f32[32,256]{1,0:T(8,128)S(1)} %get-tuple-element.203), channel_id=1, source_target_pairs={{8,16},{16,8},{24,0},{0,24},{9,17},{17,9},{25,1},{1,25},{10,18},{1... | collective-permute-start | bytes 98312 | tf_op jit(solution)/shard_map/ppermute | solution.py:30
  43.6 1.0 %collective-permute-start.22 = (f32[32,256]{1,0:T(8,128)S(1)}, f32[32,256]{1,0:T(8,128)S(1)}, u32[]{:S(2)}, u32[]{:S(2)}) collective-permute-start(f32[32,256]{1,0:T(8,128)S(1)} %get-tuple-element.204), channel_id=1, source_target_pairs={{0,8},{8,0},{16,24},{24,16},{1,9},{9,1},{17,25},{25,17},{2,10},{10... | collective-permute-start | bytes 98312 | tf_op jit(solution)/shard_map/ppermute | solution.py:30
  44.6 2.3 %block.9 = (f32[1024,256]{1,0:T(8,128)S(1)}, f32[1024,256]{1,0:T(8,128)S(1)}, f32[1024,256]{1,0:T(8,128)S(1)}, f32[1024,256]{1,0:T(8,128)S(1)}, f32[1024,256]{1,...) custom-call(bf16[1536,512]{1,0:T(8,128)(2,1)S(1)} %get-tuple-element.117.refs_0_, ...), custom_call_target="tpu_custom_call" | custom-call | flops 1610612736 | bytes 1048576 | tf_op jit(solution)/shard_map/block/pallas_call | solution.py:394
  47.5 3.3 %last.1 = (f32[1024,256]{1,0:T(8,128)}, f32[1024,256]{1,0:T(8,128)}, f32[1024,256]{1,0:T(8,128)}, f32[1024,256]{1,0:T(8,128)}, f32[1024,256]{1,0:T(8,128)}) custom-call(bf16[1536,512]{1,0:T(8,128)(2,1)S(1)} %get-tuple-element.117.refs_0_, f32[1024,256]{1,0:T(8,128)S(1)} %get-tuple-element.195.refs_1_, f32[1024,256]{1,0:T(8,128)S(1)} %get-tuple-element.196.refs_2_, ...), custom_call_target="tpu_custom_call" | custom-call | flops 1610612736 | bytes 1048576 | tf_op jit(solution)/shard_map/last/pallas_call | solution.py:403
  (41 shorter events, 6.7 us)
Async XLA Ops:
  1.9 10.1 %collective-permute-start = (f32[32,256]{1,0:T(8,128)S(1)}, f32[32,256]{1,0:T(8,128)S(1)}, u32[]{:S(2)}, u32[]{:S(2)}) collective-permute-start(f32[32,256]{1,0:T(8,128)S(1)} %get-tuple-element.127), channel_id=1, source_target_pairs={{1,2},{2,1},{3,4},{4,3},{5,6},{6,5},{7,0},{0,7},{9,10},{10,9},{11,... | collective-permute-start | bytes 98312 | tf_op jit(solution)/shard_map/ppermute | solution.py:30
  6.5 5.5 %collective-permute-start.1 = (f32[32,256]{1,0:T(8,128)S(1)}, f32[32,256]{1,0:T(8,128)S(1)}, u32[]{:S(2)}, u32[]{:S(2)}) collective-permute-start(f32[32,256]{1,0:T(8,128)S(1)} %get-tuple-element.128), channel_id=1, source_target_pairs={{8,16},{16,8},{24,0},{0,24},{9,17},{17,9},{25,1},{1,25},{10,18},{1... | collective-permute-start | bytes 98312 | tf_op jit(solution)/shard_map/ppermute | solution.py:30
  8.9 3.9 %collective-permute-start.2 = (f32[32,256]{1,0:T(8,128)S(1)}, f32[32,256]{1,0:T(8,128)S(1)}, u32[]{:S(2)}, u32[]{:S(2)}) collective-permute-start(f32[32,256]{1,0:T(8,128)S(1)} %get-tuple-element.129), channel_id=1, source_target_pairs={{0,8},{8,0},{16,24},{24,16},{1,9},{9,1},{17,25},{25,17},{2,10},{10... | collective-permute-start | bytes 98312 | tf_op jit(solution)/shard_map/ppermute | solution.py:30
  9.4 3.4 %collective-permute-start.3 = (f32[32,256]{1,0:T(8,128)S(1)}, f32[32,256]{1,0:T(8,128)S(1)}, u32[]{:S(2)}, u32[]{:S(2)}) collective-permute-start(f32[32,256]{1,0:T(8,128)S(1)} %get-tuple-element.130), channel_id=1, source_target_pairs={{0,1},{1,0},{2,3},{3,2},{4,5},{5,4},{6,7},{7,6},{8,9},{9,8},{10,11... | collective-permute-start | bytes 98312 | tf_op jit(solution)/shard_map/ppermute | solution.py:30
  13.5 5.2 %collective-permute-start.4 = (f32[32,256]{1,0:T(8,128)S(1)}, f32[32,256]{1,0:T(8,128)S(1)}, u32[]{:S(2)}, u32[]{:S(2)}) collective-permute-start(f32[32,256]{1,0:T(8,128)S(1)} %get-tuple-element.142), channel_id=1, source_target_pairs={{1,2},{2,1},{3,4},{4,3},{5,6},{6,5},{7,0},{0,7},{9,10},{10,9},{11,... | collective-permute-start | bytes 98312 | tf_op jit(solution)/shard_map/ppermute | solution.py:30
  13.5 5.1 %collective-permute-start.5 = (f32[32,256]{1,0:T(8,128)S(1)}, f32[32,256]{1,0:T(8,128)S(1)}, u32[]{:S(2)}, u32[]{:S(2)}) collective-permute-start(f32[32,256]{1,0:T(8,128)S(1)} %get-tuple-element.143), channel_id=1, source_target_pairs={{8,16},{16,8},{24,0},{0,24},{9,17},{17,9},{25,1},{1,25},{10,18},{1... | collective-permute-start | bytes 98312 | tf_op jit(solution)/shard_map/ppermute | solution.py:30
  14.9 3.9 %collective-permute-start.6 = (f32[32,256]{1,0:T(8,128)S(1)}, f32[32,256]{1,0:T(8,128)S(1)}, u32[]{:S(2)}, u32[]{:S(2)}) collective-permute-start(f32[32,256]{1,0:T(8,128)S(1)} %get-tuple-element.144), channel_id=1, source_target_pairs={{0,8},{8,0},{16,24},{24,16},{1,9},{9,1},{17,25},{25,17},{2,10},{10... | collective-permute-start | bytes 98312 | tf_op jit(solution)/shard_map/ppermute | solution.py:30
  15.6 3.2 %collective-permute-start.7 = (f32[32,256]{1,0:T(8,128)S(1)}, f32[32,256]{1,0:T(8,128)S(1)}, u32[]{:S(2)}, u32[]{:S(2)}) collective-permute-start(f32[32,256]{1,0:T(8,128)S(1)} %get-tuple-element.145), channel_id=1, source_target_pairs={{0,1},{1,0},{2,3},{3,2},{4,5},{5,4},{6,7},{7,6},{8,9},{9,8},{10,11... | collective-permute-start | bytes 98312 | tf_op jit(solution)/shard_map/ppermute | solution.py:30
  19.3 7.4 %collective-permute-start.8 = (f32[32,256]{1,0:T(8,128)S(1)}, f32[32,256]{1,0:T(8,128)S(1)}, u32[]{:S(2)}, u32[]{:S(2)}) collective-permute-start(f32[32,256]{1,0:T(8,128)S(1)} %get-tuple-element.157), channel_id=1, source_target_pairs={{1,2},{2,1},{3,4},{4,3},{5,6},{6,5},{7,0},{0,7},{9,10},{10,9},{11,... | collective-permute-start | bytes 98312 | tf_op jit(solution)/shard_map/ppermute | solution.py:30
  21.4 5.3 %collective-permute-start.9 = (f32[32,256]{1,0:T(8,128)S(1)}, f32[32,256]{1,0:T(8,128)S(1)}, u32[]{:S(2)}, u32[]{:S(2)}) collective-permute-start(f32[32,256]{1,0:T(8,128)S(1)} %get-tuple-element.158), channel_id=1, source_target_pairs={{8,16},{16,8},{24,0},{0,24},{9,17},{17,9},{25,1},{1,25},{10,18},{1... | collective-permute-start | bytes 98312 | tf_op jit(solution)/shard_map/ppermute | solution.py:30
  23.1 3.9 %collective-permute-start.10 = (f32[32,256]{1,0:T(8,128)S(1)}, f32[32,256]{1,0:T(8,128)S(1)}, u32[]{:S(2)}, u32[]{:S(2)}) collective-permute-start(f32[32,256]{1,0:T(8,128)S(1)} %get-tuple-element.159), channel_id=1, source_target_pairs={{0,8},{8,0},{16,24},{24,16},{1,9},{9,1},{17,25},{25,17},{2,10},{10... | collective-permute-start | bytes 98312 | tf_op jit(solution)/shard_map/ppermute | solution.py:30
  24.4 2.6 %collective-permute-start.11 = (f32[32,256]{1,0:T(8,128)S(1)}, f32[32,256]{1,0:T(8,128)S(1)}, u32[]{:S(2)}, u32[]{:S(2)}) collective-permute-start(f32[32,256]{1,0:T(8,128)S(1)} %get-tuple-element.160), channel_id=1, source_target_pairs={{0,1},{1,0},{2,3},{3,2},{4,5},{5,4},{6,7},{7,6},{8,9},{9,8},{10,11... | collective-permute-start | bytes 98312 | tf_op jit(solution)/shard_map/ppermute | solution.py:30
  27.5 5.2 %collective-permute-start.12 = (f32[32,256]{1,0:T(8,128)S(1)}, f32[32,256]{1,0:T(8,128)S(1)}, u32[]{:S(2)}, u32[]{:S(2)}) collective-permute-start(f32[32,256]{1,0:T(8,128)S(1)} %get-tuple-element.172), channel_id=1, source_target_pairs={{1,2},{2,1},{3,4},{4,3},{5,6},{6,5},{7,0},{0,7},{9,10},{10,9},{11,... | collective-permute-start | bytes 98312 | tf_op jit(solution)/shard_map/ppermute | solution.py:30
  28.3 4.8 %collective-permute-start.13 = (f32[32,256]{1,0:T(8,128)S(1)}, f32[32,256]{1,0:T(8,128)S(1)}, u32[]{:S(2)}, u32[]{:S(2)}) collective-permute-start(f32[32,256]{1,0:T(8,128)S(1)} %get-tuple-element.173), channel_id=1, source_target_pairs={{8,16},{16,8},{24,0},{0,24},{9,17},{17,9},{25,1},{1,25},{10,18},{1... | collective-permute-start | bytes 98312 | tf_op jit(solution)/shard_map/ppermute | solution.py:30
  29.2 3.9 %collective-permute-start.14 = (f32[32,256]{1,0:T(8,128)S(1)}, f32[32,256]{1,0:T(8,128)S(1)}, u32[]{:S(2)}, u32[]{:S(2)}) collective-permute-start(f32[32,256]{1,0:T(8,128)S(1)} %get-tuple-element.174), channel_id=1, source_target_pairs={{0,8},{8,0},{16,24},{24,16},{1,9},{9,1},{17,25},{25,17},{2,10},{10... | collective-permute-start | bytes 98312 | tf_op jit(solution)/shard_map/ppermute | solution.py:30
  30.3 2.9 %collective-permute-start.15 = (f32[32,256]{1,0:T(8,128)S(1)}, f32[32,256]{1,0:T(8,128)S(1)}, u32[]{:S(2)}, u32[]{:S(2)}) collective-permute-start(f32[32,256]{1,0:T(8,128)S(1)} %get-tuple-element.175), channel_id=1, source_target_pairs={{0,1},{1,0},{2,3},{3,2},{4,5},{5,4},{6,7},{7,6},{8,9},{9,8},{10,11... | collective-permute-start | bytes 98312 | tf_op jit(solution)/shard_map/ppermute | solution.py:30
  33.7 7.1 %collective-permute-start.16 = (f32[32,256]{1,0:T(8,128)S(1)}, f32[32,256]{1,0:T(8,128)S(1)}, u32[]{:S(2)}, u32[]{:S(2)}) collective-permute-start(f32[32,256]{1,0:T(8,128)S(1)} %get-tuple-element.187), channel_id=1, source_target_pairs={{1,2},{2,1},{3,4},{4,3},{5,6},{6,5},{7,0},{0,7},{9,10},{10,9},{11,... | collective-permute-start | bytes 98312 | tf_op jit(solution)/shard_map/ppermute | solution.py:30
  35.7 5.0 %collective-permute-start.17 = (f32[32,256]{1,0:T(8,128)S(1)}, f32[32,256]{1,0:T(8,128)S(1)}, u32[]{:S(2)}, u32[]{:S(2)}) collective-permute-start(f32[32,256]{1,0:T(8,128)S(1)} %get-tuple-element.188), channel_id=1, source_target_pairs={{8,16},{16,8},{24,0},{0,24},{9,17},{17,9},{25,1},{1,25},{10,18},{1... | collective-permute-start | bytes 98312 | tf_op jit(solution)/shard_map/ppermute | solution.py:30
  37.8 3.9 %collective-permute-start.18 = (f32[32,256]{1,0:T(8,128)S(1)}, f32[32,256]{1,0:T(8,128)S(1)}, u32[]{:S(2)}, u32[]{:S(2)}) collective-permute-start(f32[32,256]{1,0:T(8,128)S(1)} %get-tuple-element.189), channel_id=1, source_target_pairs={{0,8},{8,0},{16,24},{24,16},{1,9},{9,1},{17,25},{25,17},{2,10},{10... | collective-permute-start | bytes 98312 | tf_op jit(solution)/shard_map/ppermute | solution.py:30
  38.4 3.2 %collective-permute-start.19 = (f32[32,256]{1,0:T(8,128)S(1)}, f32[32,256]{1,0:T(8,128)S(1)}, u32[]{:S(2)}, u32[]{:S(2)}) collective-permute-start(f32[32,256]{1,0:T(8,128)S(1)} %get-tuple-element.190), channel_id=1, source_target_pairs={{0,1},{1,0},{2,3},{3,2},{4,5},{5,4},{6,7},{7,6},{8,9},{9,8},{10,11... | collective-permute-start | bytes 98312 | tf_op jit(solution)/shard_map/ppermute | solution.py:30
  42.2 5.2 %collective-permute-start.20 = (f32[32,256]{1,0:T(8,128)S(1)}, f32[32,256]{1,0:T(8,128)S(1)}, u32[]{:S(2)}, u32[]{:S(2)}) collective-permute-start(f32[32,256]{1,0:T(8,128)S(1)} %get-tuple-element.202), channel_id=1, source_target_pairs={{1,2},{2,1},{3,4},{4,3},{5,6},{6,5},{7,0},{0,7},{9,10},{10,9},{11,... | collective-permute-start | bytes 98312 | tf_op jit(solution)/shard_map/ppermute | solution.py:30
  42.6 4.8 %collective-permute-start.21 = (f32[32,256]{1,0:T(8,128)S(1)}, f32[32,256]{1,0:T(8,128)S(1)}, u32[]{:S(2)}, u32[]{:S(2)}) collective-permute-start(f32[32,256]{1,0:T(8,128)S(1)} %get-tuple-element.203), channel_id=1, source_target_pairs={{8,16},{16,8},{24,0},{0,24},{9,17},{17,9},{25,1},{1,25},{10,18},{1... | collective-permute-start | bytes 98312 | tf_op jit(solution)/shard_map/ppermute | solution.py:30
  43.6 3.9 %collective-permute-start.22 = (f32[32,256]{1,0:T(8,128)S(1)}, f32[32,256]{1,0:T(8,128)S(1)}, u32[]{:S(2)}, u32[]{:S(2)}) collective-permute-start(f32[32,256]{1,0:T(8,128)S(1)} %get-tuple-element.204), channel_id=1, source_target_pairs={{0,8},{8,0},{16,24},{24,16},{1,9},{9,1},{17,25},{25,17},{2,10},{10... | collective-permute-start | bytes 98312 | tf_op jit(solution)/shard_map/ppermute | solution.py:30
  44.6 2.9 %collective-permute-start.23 = (f32[32,256]{1,0:T(8,128)S(1)}, f32[32,256]{1,0:T(8,128)S(1)}, u32[]{:S(2)}, u32[]{:S(2)}) collective-permute-start(f32[32,256]{1,0:T(8,128)S(1)} %get-tuple-element.205), channel_id=1, source_target_pairs={{0,1},{1,0},{2,3},{3,2},{4,5},{5,4},{6,7},{7,6},{8,9},{9,8},{10,11... | collective-permute-start | bytes 98312 | tf_op jit(solution)/shard_map/ppermute | solution.py:30
  (2 other events, 13.7 us)
